TPU v7x, 32 devices: a whole 2x2x4 slice. The times are simulated.
32 devices in a mesh: slab: 4 (over x, core), img: 8 (over z, y).
Axes of the slice: x: 2, y: 2, z: 4, core: 2. Of those that a mesh axis runs over, the one named last changes fastest.
Arguments:
- feats: bfloat16 [8, 32, 128, 512], P('img', 'slab'), may hold values from -6 to 6
- labels: int32 [8], P('img'), may hold values from 0 to 999
- conv_w: bfloat16 [9, 512, 4], replicated, may hold values from -0.09375 to 0.09375
- embed_w: bfloat16 [16, 1024], replicated, may hold values from -1.5 to 1.5
- mod_table: bfloat16 [1000, 2048], replicated, may hold values from -3 to 3
- qkv_w: bfloat16 [1024, 3072], replicated, may hold values from -0.1875 to 0.1875
- out_w: bfloat16 [1024, 1024], replicated, may hold values from -0.1875 to 0.1875
- proj_w: bfloat16 [1024, 768], replicated, may hold values from -0.1875 to 0.1875
- dino: bfloat16 [8, 1024, 768], P('img', 'slab'), may hold values from -6 to 6
Outputs:
- grad_feats: bfloat16 [8, 32, 128, 512], P('img', 'slab')
- grad_proj: float32 [1024, 768], replicated
- grad_conv: float32 [9, 512, 4], replicated
- loss: float32 [], replicated
All inputs are finite; a program needn't handle non-finite values.
Results may differ from a plain program's by a relative error of at most 0.024.
Values may be sent and summed in bfloat16 or wider, within the bound.
A program may use at most 128 MiB of HBM per device.

v0:
```python
import functools
import math

import jax
import jax.numpy as jnp
from jax import lax
from jax.experimental import pallas as pl
from jax.experimental.pallas import tpu as pltpu
from jax.sharding import PartitionSpec as P

HEAD_DIM = 64
PAIR = 2 * HEAD_DIM

latent_scale = 0.18215
norm_eps = 1e-06
cosine_eps = 1e-06

MESH_ID = pl.DeviceIdType.MESH


def mm(left, right, dims, kind=jnp.float32):
    return lax.dot_general(left, right, (dims, ((), ())), preferred_element_type=kind)


def contract_first(left, right):
    return mm(left, right, ((0,), (0,)))


def contract_last(left, right):
    return mm(left, right, ((1,), (1,)))


def attend_kernel(q_ref, k_ref, v_ref, o_ref, lse_ref):
    scale = HEAD_DIM ** (-0.5)
    outs = []
    for h in range(2):
        cut = slice(h * HEAD_DIM, (h + 1) * HEAD_DIM)
        s = contract_last(k_ref[:, cut], q_ref[:, cut] * jnp.bfloat16(scale))
        top = jnp.max(s, 0, keepdims=True)
        e = jnp.exp(s - top)
        total = jnp.sum(e, 0, keepdims=True)
        o = contract_first(v_ref[:, cut], e.astype(jnp.bfloat16)) / total
        lse_ref[0, h : h + 1, :] = top + jnp.log(total)
        outs.append(o)
    o_ref[...] = jnp.concatenate(outs, 0).T.astype(jnp.bfloat16)


def attend_back_kernel(q_ref, k_ref, v_ref, g_ref, o_ref, lse_ref, gq_ref, gk_ref, gv_ref):
    scale = HEAD_DIM ** (-0.5)
    prod = (g_ref[...].astype(jnp.float32) * o_ref[...].astype(jnp.float32)).T
    gqs = []
    for h in range(2):
        cut = slice(h * HEAD_DIM, (h + 1) * HEAD_DIM)
        qs = q_ref[:, cut] * jnp.bfloat16(scale)
        k = k_ref[:, cut]
        g = g_ref[:, cut]
        delta = jnp.sum(prod[cut], 0, keepdims=True)
        p = jnp.exp(contract_last(k, qs) - lse_ref[0, h : h + 1, :])
        ds = (p * (contract_last(v_ref[:, cut], g) - delta)).astype(jnp.bfloat16)
        gk_ref[:, cut] = mm(ds, qs, ((1,), (0,))).astype(jnp.bfloat16)
        gv_ref[:, cut] = mm(p.astype(jnp.bfloat16), g, ((1,), (0,))).astype(jnp.bfloat16)
        gqs.append(contract_first(k, ds) * scale)
    gq_ref[...] = jnp.concatenate(gqs, 0).T.astype(jnp.bfloat16)


def attend(query, kv):
    count, width = query.shape
    full = kv.shape[0]
    pairs = width // PAIR
    cost = pl.CostEstimate(
        flops=4 * count * full * width, bytes_accessed=2 * (2 * full + 2 * count) * width,
        transcendentals=count * full * width // HEAD_DIM)
    return pl.pallas_call(
        attend_kernel,
        grid=(pairs,),
        in_specs=[
            pl.BlockSpec((count, PAIR), lambda i: (0, i)),
            pl.BlockSpec((full, PAIR), lambda i: (0, i)),
            pl.BlockSpec((full, PAIR), lambda i: (0, i + pairs)),
        ],
        out_specs=[
            pl.BlockSpec((count, PAIR), lambda i: (0, i)),
            pl.BlockSpec((1, 2, count), lambda i: (i, 0, 0)),
        ],
        out_shape=[
            jax.ShapeDtypeStruct((count, width), jnp.bfloat16),
            jax.ShapeDtypeStruct((pairs, 2, count), jnp.float32),
        ],
        cost_estimate=cost,
        name="attend",
    )(query, kv, kv)


def attend_back(query, kv, grad, attended, lse):
    count, width = query.shape
    full = kv.shape[0]
    pairs = width // PAIR
    cost = pl.CostEstimate(
        flops=10 * count * full * width, bytes_accessed=2 * (4 * full + 4 * count) * width,
        transcendentals=count * full * width // HEAD_DIM)
    small = pl.BlockSpec((count, PAIR), lambda i: (0, i))
    large = pl.BlockSpec((full, PAIR), lambda i: (0, i))
    return pl.pallas_call(
        attend_back_kernel,
        grid=(pairs,),
        in_specs=[
            small,
            large,
            pl.BlockSpec((full, PAIR), lambda i: (0, i + pairs)),
            small,
            small,
            pl.BlockSpec((1, 2, count), lambda i: (i, 0, 0)),
        ],
        out_specs=[small, large, large],
        out_shape=[
            jax.ShapeDtypeStruct((count, width), jnp.bfloat16),
            jax.ShapeDtypeStruct((full, width), jnp.bfloat16),
            jax.ShapeDtypeStruct((full, width), jnp.bfloat16),
        ],
        cost_estimate=cost,
        name="attend_back",
    )(query, kv, kv, grad, attended, lse)


def reduce_kernel(chips, images, *refs):
    size = (len(refs) - 8) // 5
    xs, outs, near, half, recv = (refs[i * size : (i + 1) * size] for i in range(5))
    send0, recv0, send1, recv1, send2, recv2, send3, recv3 = refs[5 * size :]
    slab = lax.axis_index("slab")
    image = lax.axis_index("img")
    core = lax.rem(slab, 2)
    me = (slab // 2) * images + image
    partner = {"slab": slab + 1 - 2 * core, "img": image}

    def spot(peer):
        return {"slab": (peer // images) * 2 + core, "img": lax.rem(peer, images)}

    def each(body):
        def run(step, _):
            body(lax.rem(me + step, chips))
            return 0

        lax.fori_loop(1, chips, run, 0)

    def copy(src, dst, send, recv_sem, device):
        return pltpu.make_async_remote_copy(
            src_ref=src, dst_ref=dst, send_sem=send, recv_sem=recv_sem,
            device_id=device, device_id_type=MESH_ID)

    barrier = pltpu.get_barrier_semaphore()
    pl.semaphore_signal(barrier, inc=1, device_id=partner, device_id_type=MESH_ID)
    each(
        lambda peer: pl.semaphore_signal(
            barrier, inc=1, device_id=spot(peer), device_id_type=MESH_ID
        )
    )
    pl.semaphore_wait(barrier, chips)

    first = [
        copy(xs[i].at[1 - core], near[i], send0.at[i], recv0.at[i], partner) for i in range(size)
    ]
    for c in first:
        c.start()
    for i in range(size):
        first[i].wait_recv()
        kind = half[i].dtype

        def add(j, _, i=i, kind=kind):
            both = xs[i][core, j].astype(jnp.float32) + near[i][j].astype(jnp.float32)
            half[i][j] = both.astype(kind)
            return 0

        lax.fori_loop(0, chips, add, 0)
        each(
            lambda peer, i=i: copy(
                half[i].at[peer], recv[i].at[me], send1.at[i, peer], recv1.at[i, me], spot(peer)
            ).start()
        )
    for i in range(size):
        each(
            lambda peer, i=i: copy(
                half[i].at[peer], recv[i].at[peer], send1.at[i, peer], recv1.at[i, peer],
                spot(peer),
            ).wait_recv()
        )
        total = lax.fori_loop(
            1,
            chips,
            lambda step, acc, i=i: acc + recv[i][lax.rem(me + step, chips)].astype(jnp.float32),
            half[i][me].astype(jnp.float32),
        )
        outs[i][core, me] = total.astype(outs[i].dtype)
        each(
            lambda peer, i=i: copy(
                outs[i].at[core, me], outs[i].at[core, me], send2.at[i, peer], recv2.at[i, me],
                spot(peer),
            ).start()
        )
    last = [
        copy(outs[i].at[core], outs[i].at[core], send3.at[i], recv3.at[i], partner)
        for i in range(size)
    ]
    for i in range(size):
        each(
            lambda peer, i=i: copy(
                outs[i].at[core, me], outs[i].at[core, peer], send2.at[i, peer],
                recv2.at[i, peer], spot(peer),
            ).wait_recv()
        )
        last[i].start()
    for i in range(size):
        first[i].wait_send()
        each(
            lambda peer, i=i: copy(
                half[i].at[peer], recv[i].at[me], send1.at[i, peer], recv1.at[i, me], spot(peer)
            ).wait_send()
        )
        each(
            lambda peer, i=i: copy(
                outs[i].at[core, me], outs[i].at[core, me], send2.at[i, peer], recv2.at[i, me],
                spot(peer),
            ).wait_send()
        )
        copy(
            outs[i].at[core], outs[i].at[1 - core], send3.at[i], recv3.at[i], partner
        ).wait_recv()
        last[i].wait_send()


def reduce_all(big, flat, slabs, images):
    chips = slabs * images // 2
    rows = math.ceil(flat.size / (2 * chips) / 1024) * 8
    cells = jnp.pad(flat, (0, 2 * chips * rows * 128 - flat.size))
    cells = cells.reshape(2, chips, rows, 128)
    parts = [big.reshape(2, chips, -1, big.shape[1]), cells]
    vmem = pl.BlockSpec(memory_space=pltpu.VMEM)
    shapes = [(p.shape, p.dtype) for p in parts]
    dma = pltpu.SemaphoreType.DMA
    out = pl.pallas_call(
        functools.partial(reduce_kernel, chips, images),
        out_shape=[jax.ShapeDtypeStruct(*s) for s in shapes],
        in_specs=[vmem] * 2,
        out_specs=[vmem] * 2,
        scratch_shapes=[pltpu.VMEM(s[1:], k) for s, k in shapes] * 3
        + [dma((2,))] * 2
        + [dma((2, chips))] * 4
        + [dma((2,))] * 2,
        compiler_params=pltpu.CompilerParams(collective_id=0, has_side_effects=True),
        name="reduce_all",
    )(*parts)
    return out[0].reshape(big.shape), out[1].reshape(-1)[: flat.size]


def cosine_grad(projected, target):
    norm_p = jnp.sqrt(jnp.sum(projected * projected, -1, keepdims=True) + cosine_eps)
    norm_t = jnp.sqrt(jnp.sum(target * target, -1, keepdims=True) + cosine_eps)
    cosine = jnp.sum(projected * target, -1, keepdims=True) / (norm_p * norm_t)
    grad = cosine * projected / (norm_p * norm_p) - target / (norm_p * norm_t)
    return (cosine[:, 0], grad)


def local(feats, labels, conv_w, embed_w, mod_table, qkv_w, out_w, proj_w, dino):
    image = feats[0]
    rows, cols, chans = image.shape
    outs = conv_w.shape[2]
    width = qkv_w.shape[0]
    slabs = lax.axis_size("slab")
    images = lax.axis_size("img")
    slab = lax.axis_index("slab")
    cells = image.reshape(rows * cols, chans)
    taps = conv_w.transpose(0, 2, 1).reshape(9 * outs, chans)
    resp = contract_last(taps, cells).reshape(3, 3, outs, rows, cols)
    resp = jnp.pad(resp, ((0, 0), (0, 0), (0, 0), (0, 0), (1, 1)))
    flat = sum(resp[:, kx, :, :, kx : kx + cols] for kx in range(3))
    terms = sum(
        jnp.pad(flat[ky], ((0, 0), (2 - ky, ky), (0, 0))) for ky in range(3)
    )
    terms_all = lax.all_gather(terms, "slab", axis=0)
    full_rows = rows * slabs
    latent = sum(
        jnp.pad(terms_all[s], ((0, 0), (s * rows, full_rows - (s + 1) * rows), (0, 0)))
        for s in range(slabs)
    )[:, 1:-1] * latent_scale
    tokens = latent.reshape(outs, full_rows // 2, 2, cols // 2, 2).transpose(1, 3, 2, 4, 0)
    tokens = tokens.reshape(-1, 4 * outs)
    full = tokens.shape[0]
    count = full // slabs
    own = slab * count
    high = lax.reduce_precision(tokens, 8, 7)
    mid = lax.reduce_precision(tokens - high, 8, 7)
    low = tokens - high - mid
    split = jnp.concatenate([high, mid, low], 1).astype(jnp.bfloat16)
    start = jnp.dot(
        split, jnp.concatenate([embed_w] * 3, 0), preferred_element_type=jnp.float32
    )
    row = lax.dynamic_index_in_dim(mod_table, labels[0], 0, keepdims=False).astype(jnp.float32)
    gain = 1.0 + row[width:]
    mean = jnp.mean(start, -1, keepdims=True)
    cent = start - mean
    inv = lax.rsqrt(jnp.mean(cent * cent, -1, keepdims=True) + norm_eps)
    normed = cent * inv
    modded = (normed * gain + row[:width]).astype(jnp.bfloat16)

    def mine(whole):
        return lax.dynamic_slice_in_dim(whole, own, count, 0)

    kv = jnp.dot(modded, qkv_w[:, width:], preferred_element_type=jnp.float32).astype(jnp.bfloat16)
    query = jnp.dot(
        mine(modded), qkv_w[:, :width], preferred_element_type=jnp.float32
    ).astype(jnp.bfloat16)
    attended, lse = attend(query, kv)
    resid = mine(start) + jnp.dot(attended, out_w, preferred_element_type=jnp.float32)
    resid_b = resid.astype(jnp.bfloat16)
    projected = jnp.dot(resid_b, proj_w, preferred_element_type=jnp.float32)
    cosine, grad_p = cosine_grad(projected, dino[0].astype(jnp.float32))
    grad_pb = grad_p.astype(jnp.bfloat16)
    proj_part = contract_first(resid_b, grad_pb).astype(jnp.bfloat16)
    grad_resid = contract_last(grad_pb, proj_w)
    grad_att = contract_last(grad_resid.astype(jnp.bfloat16), out_w).astype(jnp.bfloat16)
    grad_query, grad_key, grad_value = attend_back(query, kv, grad_att, attended, lse)

    def norm_back(grad_mod, inv, normed):
        grad_norm = grad_mod * gain
        return inv * (
            grad_norm
            - jnp.mean(grad_norm, -1, keepdims=True)
            - normed * jnp.mean(grad_norm * normed, -1, keepdims=True)
        )

    grad_mod = contract_last(grad_key, qkv_w[:, width : 2 * width]) + contract_last(
        grad_value, qkv_w[:, 2 * width :]
    )
    spread = contract_last(embed_w, norm_back(grad_mod, inv, normed).astype(jnp.bfloat16))
    grad_own = grad_resid + norm_back(
        contract_last(grad_query, qkv_w[:, :width]), mine(inv), mine(normed)
    )
    spread_own = contract_last(embed_w, grad_own.astype(jnp.bfloat16))
    spread = spread + lax.dynamic_update_slice_in_dim(
        jnp.zeros_like(spread), spread_own, own, 1
    )
    grad_tokens = jnp.sum(lax.all_gather(spread, "slab", axis=0), 0)
    grad_latent = grad_tokens.reshape(2, 2, outs, full_rows // 2, cols // 2)
    grad_latent = grad_latent.transpose(3, 0, 2, 4, 1).reshape(full_rows, outs, cols)
    grad_latent = (grad_latent * latent_scale).astype(jnp.bfloat16)
    grad_pad = lax.dynamic_slice_in_dim(
        jnp.pad(grad_latent, ((1, 1), (0, 0), (1, 1))), slab * rows, rows + 2, 0
    )
    sides = jnp.concatenate([grad_pad[:, :, 2 - kx : 2 - kx + cols] for kx in range(3)], 1)
    views = jnp.concatenate([sides[2 - ky : 2 - ky + rows] for ky in range(3)], 1)
    grad_image = mm(views, taps, ((1,), (0,))).astype(jnp.bfloat16)[None]
    conv_part = mm(views, image, ((0, 2), (0, 1)))
    loss_part = jnp.sum(1.0 - cosine)
    proj_sum, summed = reduce_all(
        proj_part, jnp.concatenate([conv_part.reshape(-1), loss_part[None]]), slabs, images
    )
    grad_proj = proj_sum.astype(jnp.float32)
    grad_conv = summed[:-1].reshape(9, outs, chans).transpose(0, 2, 1)
    return (grad_image, grad_proj, grad_conv, summed[-1] / (slabs * images * count))


def solution(mesh):
    in_specs = (
        P("img", "slab", None, None),
        P("img"),
        P(),
        P(),
        P(),
        P(),
        P(),
        P(),
        P("img", "slab", None),
    )
    out_specs = (P("img", "slab", None, None), P(), P(), P())
    return jax.shard_map(local, mesh=mesh, in_specs=in_specs, out_specs=out_specs, check_vma=False)
```

profile of v0, /device:TPU:0, one launch (start us, length us, event | category | flops | bytes accessed | tf_op | source)
XLA Modules:
  0.0 164.8 jit_solution(3091720854527591926)
XLA Ops:
  0.6 0.0 copy-start
  0.6 0.0 copy-start.10
  0.7 1.8 %fusion.26 = f32[3,3,4,8,128]{4,2,3,1,0:T(4,128)S(1)} fusion(bf16[3,3,4,512,1]{3,2,4,1,0:T(4,128)(2,1)} %bitcast.90, bf16[1,8,128,512]{3,2,1,0:T(8,128)(2,1)} %param.9), kind=kOutput, calls=%fused_computation.34 | convolution fusion | flops 37748736 | bytes 1232896 | tf_op jit(solution)/shard_map/dot_general | solution.py:22
  2.5 0.1 fusion.52
  2.6 6.5 %all-gather = f32[16,10,128]{2,1,0:T(8,128)S(1)} all-gather(f32[4,10,128]{2,1,0:T(8,128)S(1)} %copy.23), channel_id=2, replica_groups=mesh['slab'=4,'img'=8] {'slab'}, dimensions={0}, use_global_device_ids=true | all-gather | bytes 102400 | tf_op jit(solution)/shard_map/all_gather | solution.py:278
  9.2 2.0 %copy.24 = f32[4,32,128]{0,2,1:T(8,128)} copy(f32[4,32,128]{2,1,0:T(8,128)S(1)} %fusion.50) | data formatting | bytes 131072 | tf_op jit(solution)/shard_map/mul | solution.py:280
  11.2 2.8 %copy.25 = f32[16,64,2,2,4]{1,0,4,3,2:T(8,128)S(1)} copy(f32[16,64,2,2,4]{4,3,1,2,0:T(2,128)} %bitcast.84) | data formatting | bytes 131072 | tf_op jit(solution)/shard_map/transpose | solution.py:284
  13.9 0.1 reshape.139
  14.1 0.0 copy-done.10
  14.1 0.8 fusion.63
  14.9 0.0 copy-start.2
  14.9 2.0 %copy-done.2 = f32[1024,1024]{0,1:T(8,128)} copy-done((f32[1024,1024]{0,1:T(8,128)}, f32[1024,1024]{0,1:T(8,128)S(1)}, u32[]{:S(2)}) %copy-start.2) | copy-done | bytes 4194328
  16.8 0.5 multiply_reduce_fusion.1
  18.0 0.8 dynamic-slice_convert_fusion
  18.8 4.8 %add_convert_fusion = (bf16[1024,1024]{0,1:T(8,128)(2,1)S(1)}, f32[1024,1024]{0,1:T(8,128)}) fusion(f32[1024]{0:T(1024)S(1)} %bitcast.96, f32[1024]{0:T(1024)S(1)} %bitcast.93, f32[1024]{0:T(1024)S(1)} %add_rsqrt_fusion, f32[1024,1024]{0,1:T(8,128)} %copy-done.2, f32[1024]{0:T(1024)S(1)} %broadcast_multiply_fusion.2), kind=kLoop, calls=%fused_computation.5 | loop fusion | flops 5242880 | bytes 10502144 | tf_op jit(solution)/shard_map/convert_element_type | solution.py:302
  23.6 9.1 %fusion.2.k_ref.v_ref = bf16[1024,2048]{1,0:T(8,128)(2,1)} fusion(bf16[1024,1024]{0,1:T(8,128)(2,1)S(1)} %get-tuple-element.28, bf16[1024,3072]{1,0:T(8,128)(2,1)} %param.14), kind=kOutput, calls=%fused_computation.8 | convolution fusion | flops 4297064448 | bytes 10485760 | tf_op jit(solution)/shard_map/dot_general | solution.py:307
  32.7 0.0 copy-done.7
  32.7 3.3 %fusion.20.q_ref = bf16[256,1024]{1,0:T(8,128)(2,1)} fusion(bf16[1024,3072]{1,0:T(8,128)(2,1)} %param.14, bf16[1024,1024]{0,1:T(8,128)(2,1)} %copy-done.7, s32[]{:T(128)S(6)} %select_n.15), kind=kOutput, calls=%fused_computation.24 | convolution fusion | flops 537133056 | bytes 3145732 | tf_op jit(solution)/shard_map/dot_general | solution.py:308
  36.0 14.3 %attend.1 = (bf16[256,1024]{1,0:T(8,128)(2,1)}, f32[8,2,256]{2,1,0:T(2,128)}) custom-call(bf16[256,1024]{1,0:T(8,128)(2,1)} %fusion.20.q_ref, bf16[1024,2048]{1,0:T(8,128)(2,1)} %fusion.2.k_ref.v_ref, bf16[1024,2048]{1,0:T(8,128)(2,1)} %fusion.2.k_ref.v_ref), custom_call_target="tpu_custom_call" | custom-call | flops 1073741824 | bytes 5242880 | tf_op jit(solution)/shard_map/attend/pallas_call | solution.py:73
  50.2 0.0 copy-start.3
  50.3 0.0 copy-done
  50.3 2.5 %fusion.23 = bf16[256,1024]{0,1:T(8,128)(2,1)S(1)} fusion(bf16[256,1024]{1,0:T(8,128)(2,1)} %get-tuple-element.11.o_ref, bf16[1024,1024]{1,0:T(8,128)(2,1)S(1)} %copy-done, f32[1024,1024]{0,1:T(8,128)} %copy-done.2, s32[]{:T(128)S(6)} %select_n.15), kind=kOutput, calls=%fused_computation.26 | convolution fusion | flops 537395200 | bytes 4194308 | tf_op jit(solution)/shard_map/dot_general | solution.py:312
  52.7 0.0 copy-done.3
  52.7 0.0 copy-done.8
  52.7 0.0 copy-start.5
  52.8 0.8 fusion.29
  53.6 0.6 subtract_reduce_fusion
  54.2 0.2 fusion.32
  54.4 0.6 fusion.64
  55.0 1.5 convolution_convert_fusion.2.g_ref
  56.6 0.0 copy-done.5
  56.6 14.5 %attend_back.1 = (bf16[256,1024]{1,0:T(8,128)(2,1)}, bf16[1024,1024]{1,0:T(8,128)(2,1)}, bf16[1024,1024]{1,0:T(8,128)(2,1)}) custom-call(bf16[256,1024]{1,0:T(8,128)(2,1)} %fusion.20.q_ref, bf16[1024,2048]{1,0:T(8,128)(2,1)} %fusion.2.k_ref.v_ref, bf16[1024,2048]{1,0:T(8,128)(2,1)} %fusion.2.k_ref.v_ref, bf16[256,1024]{1,0:T(8,128)(2,1)} %convolution_convert_fusion.2.g_ref, ...), custom_call_target="tpu_custom_call" | custom-call | flops 2684354560 | bytes 10485760 | tf_op jit(solution)/shard_map/attend_back/pallas_call | solution.py:103
  71.1 3.9 %fusion.60 = (f32[256]{0:T(256)S(1)}, f32[256]{0:T(256)S(1)}, f32[256,1024]{0,1:T(8,128)}) fusion(f32[1024,1024]{0,1:T(8,128)} %get-tuple-element.29, s32[]{:T(128)S(6)} %select_n.15, f32[1024]{0:T(1024)S(1)} %bitcast.94, bf16[256,1024]{1,0:T(8,128)(2,1)} %get-tuple-element.15, bf16[1024,3072]{1,0:T(8,128)(2,1)} %param.14), kind=kOutput, calls=%fused_computation.104 | convolution fusion | flops 537918976 | bytes 4724740 | tf_op jit(solution)/shard_map/dot_general | solution.py:22
  75.0 0.0 copy-done.14
  75.0 0.0 copy-start.4
  75.0 4.1 %fusion.5 = f32[1024,1024]{0,1:T(8,128)S(1)} fusion(bf16[1024,1024]{1,0:T(8,128)(2,1)S(1)} %copy-done.14, bf16[1024,3072]{1,0:T(8,128)(2,1)} %param.14), kind=kOutput, calls=%fused_computation.9 | convolution fusion | flops 2147483648 | bytes 8388608 | tf_op jit(solution)/shard_map/dot_general | solution.py:22
  79.2 0.0 copy-done.1
  79.2 0.0 copy-done.4
  79.2 0.0 copy-start.11
  79.2 4.4 %fusion.59 = (f32[1024]{0:T(1024)S(1)}, f32[1024]{0:T(1024)S(1)}, f32[1024,1024]{0,1:T(8,128)S(1)}) fusion(f32[1024,1024]{0,1:T(8,128)S(1)} %copy-done.1, f32[1024]{0:T(1024)S(1)} %bitcast.95, f32[1024,1024]{0,1:T(8,128)S(1)} %fusion.5, bf16[1024,1024]{1,0:T(8,128)(2,1)S(1)} %copy-done.4, bf16[1024,3072]{1,0:T(8,128)(2,1)} %param.14), kind=kOutput, calls=%fused_computation.103 | convolution fusion | flops 2152724480 | bytes 16789504 | tf_op jit(solution)/shard_map/dot_general | solution.py:22
  83.6 0.0 copy-done.11
  83.6 0.8 fusion.9
  84.4 0.6 copy-done.9
  85.0 0.6 copy.35
  85.6 1.3 copy.28
  86.9 0.1 dynamic-slice.5
  87.0 2.8 %fusion.25 = f32[1,16,1024]{2,1,0:T(8,128)} fusion(f32[1,16,1024]{2,1,0:T(8,128)} %copy.35, s32[]{:T(128)S(6)} %select_n.15, bf16[16,1024]{1,0:T(8,128)(2,1)} %param.12, f32[256,1024]{0,1:T(8,128)} %copy.28, f32[256,1024]{0,1:T(8,128)} %get-tuple-element.53, f32[1024,1024]{0,1:T(8,128)} %get-tuple-element.29, f32[256]{0:T(256)S(1)} %get-tuple-element.56, ...), kind=kOutput, calls=%fused_computation.33 | convolution fusion | flops 9965568 | bytes 3215360 | tf_op jit(solution)/shard_map/dot_general | solution.py:22
  89.9 6.3 %all_gather.18 = f32[4,16,1024]{2,1,0:T(8,128)S(1)} all-gather(f32[1,16,1024]{2,1,0:T(8,128)} %fusion.25), channel_id=1, replica_groups=mesh['slab'=4,'img'=8] {'slab'}, dimensions={0}, use_global_device_ids=true | all-gather | bytes 327680 | tf_op jit(solution)/shard_map/all_gather | solution.py:341
  96.2 0.1 convert_element_type.95
  96.3 2.1 %copy.29 = bf16[16,2,4,64,2]{2,4,3,1,0:T(2,128)(2,1)} copy(bf16[16,2,4,64,2]{3,0,2,4,1:T(8,128)(2,1)S(1)} %bitcast.89) | data formatting | bytes 65536 | tf_op jit(solution)/shard_map/convert_element_type | solution.py:344
  98.5 1.6 copy.30
  100.1 0.1 pad_dynamic-slice_fusion.1
  100.2 1.5 convolution_bitcast_fusion
  101.8 1.3 select_maximum_fusion
  103.1 0.0 copy-done.6
  103.1 1.7 %convolution_convert_fusion = bf16[1024,768]{1,0:T(8,128)(2,1)} fusion(bf16[256,1024]{0,1:T(8,128)(2,1)S(1)} %copy-done.6, bf16[256,768]{1,0:T(8,128)(2,1)S(1)} %fusion.32), kind=kOutput, calls=%fused_computation.18 | convolution fusion | flops 403439616 | bytes 2490368 | tf_op jit(solution)/shard_map/dot_general | solution.py:22
  104.8 52.2 %reduce_all.1 = (bf16[2,16,32,768]{3,2,1,0:T(8,128)(2,1)}, f32[2,16,8,128]{3,2,1,0:T(8,128)}) custom-call(bf16[2,16,32,768]{3,2,1,0:T(8,128)(2,1)} %bitcast.85, f32[2,16,8,128]{3,2,1,0:T(8,128)} %bitcast.87), custom_call_target="tpu_custom_call" | custom-call | tf_op jit(solution)/shard_map/reduce_all/pallas_call | solution.py:239
  157.0 0.0 copy-start.13
  157.0 3.3 %bitcast_convert_fusion = f32[1024,768]{1,0:T(8,128)} fusion(bf16[2,16,32,768]{3,2,1,0:T(8,128)(2,1)} %get-tuple-element.16), kind=kLoop, calls=%fused_computation.19 | loop fusion | flops 786432 | bytes 4718592 | tf_op jit(solution)/shard_map/convert_element_type | solution.py:356
  160.3 0.0 copy-done.13
  160.4 0.6 slice_bitcast_fusion
  161.0 0.5 slice.135
  162.2 0.0 copy-done.12
  162.2 1.5 fusion.16
  (25 shorter events, 0.3 us)
Async XLA Ops:
  0.6 49.6 %copy-start = (bf16[1024,1024]{1,0:T(8,128)(2,1)S(1)}, bf16[1024,1024]{1,0:T(8,128)(2,1)}, u32[]{:S(2)}) copy-start(bf16[1024,1024]{1,0:T(8,128)(2,1)} %param.15) | copy-start | bytes 6291460
  0.6 13.4 %copy-start.10 = (bf16[16,1024]{1,0:T(8,128)(2,1)S(1)}, bf16[16,1024]{1,0:T(8,128)(2,1)}, u32[]{:S(2)}) copy-start(bf16[16,1024]{1,0:T(8,128)(2,1)} %param.12) | copy-start | bytes 98308
  14.9 2.0 %copy-start.2 = (f32[1024,1024]{0,1:T(8,128)}, f32[1024,1024]{0,1:T(8,128)S(1)}, u32[]{:S(2)}) copy-start(f32[1024,1024]{0,1:T(8,128)S(1)} %get-tuple-element.50) | copy-start | bytes 12582916
  23.6 9.1 %copy-start.7 = (bf16[1024,1024]{0,1:T(8,128)(2,1)}, bf16[1024,1024]{0,1:T(8,128)(2,1)S(1)}, u32[]{:S(2)}) copy-start(bf16[1024,1024]{0,1:T(8,128)(2,1)S(1)} %get-tuple-element.28) | copy-start | bytes 6291460
  50.2 2.5 %copy-start.3 = (bf16[1024,768]{1,0:T(8,128)(2,1)S(1)}, bf16[1024,768]{1,0:T(8,128)(2,1)}, u32[]{:S(2)}) copy-start(bf16[1024,768]{1,0:T(8,128)(2,1)} %param.16) | copy-start | bytes 4718596
  50.2 2.5 %copy-start.8 = (bf16[1,256,768]{2,1,0:T(8,128)(2,1)S(1)}, bf16[1,256,768]{2,1,0:T(8,128)(2,1)}, u32[]{:S(2)}) copy-start(bf16[1,256,768]{2,1,0:T(8,128)(2,1)} %param.17) | copy-start | bytes 1179652
  52.7 3.8 %copy-start.5 = (bf16[256,1024]{0,1:T(8,128)(2,1)}, bf16[256,1024]{0,1:T(8,128)(2,1)S(1)}, u32[]{:S(2)}) copy-start(bf16[256,1024]{0,1:T(8,128)(2,1)S(1)} %fusion.23) | copy-start | bytes 1572868
  71.1 3.9 %copy-start.14 = (bf16[1024,1024]{1,0:T(8,128)(2,1)S(1)}, bf16[1024,1024]{1,0:T(8,128)(2,1)}, u32[]{:S(2)}) copy-start(bf16[1024,1024]{1,0:T(8,128)(2,1)} %get-tuple-element.14) | copy-start | bytes 6291460
  75.0 4.2 %copy-start.1 = (f32[1024,1024]{0,1:T(8,128)S(1)}, f32[1024,1024]{0,1:T(8,128)}, u32[]{:S(2)}) copy-start(f32[1024,1024]{0,1:T(8,128)} %get-tuple-element.29) | copy-start | bytes 12582916
  75.0 4.2 %copy-start.4 = (bf16[1024,1024]{1,0:T(8,128)(2,1)S(1)}, bf16[1024,1024]{1,0:T(8,128)(2,1)}, u32[]{:S(2)}) copy-start(bf16[1024,1024]{1,0:T(8,128)(2,1)} %get-tuple-element.13) | copy-start | bytes 6291460
  79.2 4.4 %copy-start.11 = (bf16[16,1024]{1,0:T(8,128)(2,1)S(1)}, bf16[16,1024]{1,0:T(8,128)(2,1)}, u32[]{:S(2)}) copy-start(bf16[16,1024]{1,0:T(8,128)(2,1)} %param.12) | copy-start | bytes 98308
  84.4 0.6 copy-start.9
  86.9 16.1 %copy-start.6 = (bf16[256,1024]{0,1:T(8,128)(2,1)S(1)}, bf16[256,1024]{0,1:T(8,128)(2,1)}, u32[]{:S(2)}) copy-start(bf16[256,1024]{0,1:T(8,128)(2,1)} %copy-done.5) | copy-start | bytes 1572868
  103.1 59.1 %copy-start.12 = (bf16[9,512,4]{1,2,0:T(4,128)(2,1)S(1)}, bf16[9,512,4]{1,2,0:T(4,128)(2,1)}, u32[]{:S(2)}) copy-start(bf16[9,512,4]{1,2,0:T(4,128)(2,1)} %param.11) | copy-start | bytes 110596
  157.0 3.4 %copy-start.13 = (f32[2,16,8,128]{3,2,1,0:T(8,128)S(1)}, f32[2,16,8,128]{3,2,1,0:T(8,128)}, u32[]{:S(2)}) copy-start(f32[2,16,8,128]{3,2,1,0:T(8,128)} %get-tuple-element.17) | copy-start | bytes 393220
where the time goes:
time: 165 us
  Pallas kernels  81 us (49%)
  matrix products  41 us (25%)
  local copies, waits for them, and re-layouts  14.7 us (9%)
  blocking collectives  12.8 us (8%)
  other arithmetic  11.8 us (7%)
  between operations  3.41 us (2%)
    pallas_call x1, Pallas kernels, reduce_all(): pl.pallas_call(functools.partial(reduce_kernel, chips, images), out_shape...  52.2 us
    dot_general x11, matrix products, mm(): lax.dot_general(left, right, (dims, ((), ())), preferred_element_type=kind)  24.6 us
    pallas_call x1, Pallas kernels, attend_back(): pl.pallas_call(attend_back_kernel, grid=(pairs,), in_specs=[small, large,...  14.5 us
    pallas_call x1, Pallas kernels, attend(): pl.pallas_call(attend_kernel, grid=(pairs,), in_specs=[pl.BlockSpec((coun...  14.3 us
    dot_general x1, matrix products, local(): jnp.dot(modded, qkv_w[:, width:], preferred_element_type=jnp.float32)  9.08 us
    all_gather x1, blocking collectives, local(): terms_all = lax.all_gather(terms, 'slab', axis=0)  6.51 us
    all_gather x1, blocking collectives, local(): grad_tokens = jnp.sum(lax.all_gather(spread, 'slab', axis=0), 0)  6.33 us
    convert_element_type x1, other arithmetic, local(): modded = (normed * gain + row[:width]).astype(jnp.bfloat16)  4.82 us

commit v1 on v0

v1 whole, which is shorter than its diff:
```python
import functools

import jax
import jax.numpy as jnp
from jax import lax
from jax.experimental import pallas as pl
from jax.experimental.pallas import tpu as pltpu
from jax.sharding import PartitionSpec as P

HEAD_DIM = 64
PAIR = 2 * HEAD_DIM
LANES = 128
TAPS = 48

latent_scale = 0.18215
norm_eps = 1e-06
cosine_eps = 1e-06

MESH_ID = pl.DeviceIdType.MESH
F32 = jnp.float32
BF16 = jnp.bfloat16


def mm(left, right, dims):
    return lax.dot_general(left, right, (dims, ((), ())), preferred_element_type=F32)


def plain(left, right):
    return mm(left, right, ((1,), (0,)))


def contract_first(left, right):
    return mm(left, right, ((0,), (0,)))


def contract_last(left, right):
    return mm(left, right, ((1,), (1,)))


def split2(x):
    high = x.astype(BF16)
    return high, (x - high.astype(F32)).astype(BF16)


def split3(x):
    high = x.astype(BF16)
    rest = x - high.astype(F32)
    mid = rest.astype(BF16)
    return high, mid, (rest - mid.astype(F32)).astype(BF16)


def iota(shape, dim):
    return lax.broadcasted_iota(jnp.int32, shape, dim)


def shifted(x, by):
    lane = iota(x.shape, 1)
    if by > 0:
        return jnp.where(lane == 0, 0.0, pltpu.roll(x, 1, axis=1))
    return jnp.where(lane == LANES - 1, 0.0, pltpu.roll(x, LANES - 1, axis=1))


def step_kernel(
    slabs, images,
    feats_hbm, taps_ref, embed_ref, row_ref, qkv_hbm, out_hbm, proj_hbm, dino_hbm,
    gfeat_ref, gproj_ref, gconv_ref, loss_ref,
    feats, w_own, out_w, proj_w, dino, load_sems,
    taps48, resp_g, terms, terms_all, stack, tokens, emb, xw, tstack, mt, ep,
    inv_s, gct, k_s, v_s, qt, e_s, r_s, attt, att, residb, gzp, gt_aug, gt, ds_s,
    gk_s, gv_s, gqt, yr, spread, spread_all, vs,
    cbuf, crecv, cfull, gp, gp_recv, gp_out, loss_s,
    dino_sems, t_send, t_recv, a_send, a_recv, s_send, s_recv,
    c_send, c_recv, d_send, d_recv, g_send, g_recv, h_send, h_recv, p_sems,
):
    slab = lax.axis_index("slab")
    image = lax.axis_index("img")
    core = lax.rem(slab, 2)
    chip = slab // 2
    partner = {"slab": slab + 1 - 2 * core, "img": image}
    devices = slabs * images
    chips = devices // 2
    me = slab * images + image
    my_chip = chip * images + image
    width = out_w.shape[0]
    half = width // 2
    full = tokens.shape[1]
    block = dino.shape[1]
    own = 2 * block
    npairs = half // PAIR
    f_rows = emb.shape[0]

    def anyone(j):
        return {"slab": j // images, "img": lax.rem(j, images)}

    def same_core(j):
        return {"slab": (j // images) * 2 + core, "img": lax.rem(j, images)}

    def remote(src, dst, send, recv, device):
        return pltpu.make_async_remote_copy(
            src_ref=src, dst_ref=dst, send_sem=send, recv_sem=recv,
            device_id=device, device_id_type=MESH_ID)

    def others(count, self_index, body):
        def run(step, _):
            body(lax.rem(self_index + step, count))
            return 0

        lax.fori_loop(1, count, run, 0)

    loads = [pltpu.make_async_copy(feats_hbm, feats, load_sems.at[0])]
    for j in range(3):
        loads.append(pltpu.make_async_copy(
            qkv_hbm.at[:, pl.ds(pl.multiple_of(j * width + core * half, LANES), half)],
            w_own.at[j], load_sems.at[1 + j]))
    loads.append(pltpu.make_async_copy(proj_hbm, proj_w, load_sems.at[4]))
    loads.append(pltpu.make_async_copy(out_hbm, out_w, load_sems.at[5]))
    loads.append(pltpu.make_async_copy(dino_hbm, dino.at[core], load_sems.at[6]))
    for c in loads:
        c.start()

    barrier = pltpu.get_barrier_semaphore()
    others(devices, me, lambda j: pl.semaphore_signal(
        barrier, inc=1, device_id=anyone(j), device_id_type=MESH_ID))

    vs[...] = jnp.zeros_like(vs)
    for kx in range(3):
        for ky in range(3):
            vs[kx * 16 + ky * 4 : kx * 16 + ky * 4 + 4, : feats.shape[1]] = (
                taps_ref[ky * 3 + kx].astype(F32))
    taps48[...] = vs[:, : feats.shape[1]].astype(BF16)
    for dy in range(2):
        for dx in range(2):
            emb[dx * 8 + dy * 4 : dx * 8 + dy * 4 + 4, :] = (
                embed_ref[dy * 8 + dx * 4 : dy * 8 + dx * 4 + 4, :].astype(F32))

    loads[0].wait()
    resp = contract_last(taps48[...], feats[...])
    rows = resp.shape[1] // LANES
    for r in range(rows):
        cut = slice(r * LANES, (r + 1) * LANES)
        resp_g[r] = resp[16:32, cut] + shifted(resp[0:16, cut], 1) + shifted(resp[32:48, cut], -1)
    tiles = rows // 2 + 2
    for k in range(tiles):
        for dy in range(2):
            h = 2 * (k - 1) + dy
            total = None
            for ky in range(3):
                r = h + ky - 1
                if 0 <= r < rows:
                    part = resp_g[r, ky * 4 : ky * 4 + 4, :]
                    total = part if total is None else total + part
            if total is None:
                total = jnp.zeros((4, LANES), F32)
            terms[k, dy * 4 : dy * 4 + 4, :] = total

    pl.semaphore_wait(barrier, devices - 1)
    t_copies = []
    for d in range(1, slabs):
        peer = lax.rem(slab + d, slabs)
        t_copies.append(remote(
            terms, terms_all.at[slab], t_send.at[d], t_recv.at[d], {"slab": peer, "img": image}))
    for c in t_copies:
        c.start()
    loads[6].wait()
    dino_copy = remote(dino_hbm, dino.at[core], dino_sems.at[0], dino_sems.at[1], partner)
    dino_copy.start()
    terms_all[slab] = terms[...]

    gain = 1.0 + row_ref[1:2, :]
    stack_l = jnp.concatenate(
        [emb[...] * gain, gain, row_ref[0:1, :], jnp.zeros((6, width), F32)], 0)
    parts = jnp.concatenate(split3(stack_l), 0)
    for j in range(3):
        loads[1 + j].wait()
        prod = plain(parts, w_own[j])
        xw[j] = prod[0:24] + prod[24:48] + prod[48:72]
    ebar = jnp.mean(emb[...], 1, keepdims=True)
    ecent = emb[...] - ebar
    gram = lax.dot_general(
        ecent, ecent, (((1,), (1,)), ((), ())), precision=lax.Precision.HIGHEST,
        preferred_element_type=F32)
    loads[4].wait()
    ep[...] = plain(emb[...].astype(BF16), proj_w[...])
    loads[5].wait()
    mt[...] = plain(
        out_w[pl.ds(pl.multiple_of(core * half, 8), half), :], proj_w[...]).astype(BF16)

    for c in t_copies:
        c.wait_recv()

    per = rows // 2
    for i in range(per * slabs):
        p, k = divmod(i, per)
        lat = terms_all[p, k + 1]
        if k == 0 and p > 0:
            lat = lat + terms_all[p - 1, per + 1]
        if k == per - 1 and p < slabs - 1:
            lat = lat + terms_all[p + 1, 0]
        stack[(i // 2) * 8 : (i // 2) * 8 + 8, (i % 2) * LANES : (i % 2 + 1) * LANES] = (
            lat * latent_scale)
    spots = iota((2 * LANES, 2 * LANES), 0)
    dests = iota((2 * LANES, 2 * LANES), 1)
    hit = jnp.logical_and(
        lax.shift_right_logical(spots, 7) == lax.shift_right_logical(dests & 127, 6),
        (spots & 127) == 2 * (dests & 63) + lax.shift_right_logical(dests, 7))
    select = jnp.where(hit, 1.0, 0.0).astype(BF16)
    lines = stack.shape[0]
    moved = plain(jnp.concatenate(split3(stack[...]), 0), select)
    moved = moved[0:lines] + moved[lines : 2 * lines] + moved[2 * lines :]
    for i2 in range(lines // 8):
        for dx in range(2):
            tokens[dx * 8 : dx * 8 + 8, i2 * LANES : (i2 + 1) * LANES] = (
                moved[i2 * 8 : i2 * 8 + 8, dx * LANES : (dx + 1) * LANES])
    tok = tokens[...]
    emb_b = emb[...].astype(BF16)
    tok3 = jnp.concatenate(split3(tok), 0)
    emb3 = jnp.concatenate([emb_b] * 3, 0)
    invs = []
    for b in range(full // 256):
        st = contract_first(emb3, tok3[:, b * 256 : (b + 1) * 256])
        cent = st - jnp.mean(st, 0, keepdims=True)
        invs.append(lax.rsqrt(jnp.mean(cent * cent, 0, keepdims=True) + norm_eps))
    inv = jnp.concatenate(invs, 1)
    inv_s[...] = inv
    tn = tok * inv
    tokens[...] = tn
    gct[...] = lax.dot_general(
        gram, tn, (((1,), (0,)), ((), ())), precision=lax.Precision.HIGHEST,
        preferred_element_type=F32) * (1.0 / width)
    tn_hi, tn_lo = split2(tn)
    ones = jnp.where(iota((16, full), 0) < 2, 1.0, 0.0).astype(BF16)
    tstack[...] = jnp.concatenate([tn_hi, tn_hi, tn_lo, ones], 0)

    def basis(j):
        b = xw[j, 0:16, :] - ebar * xw[j, 16:17, :]
        b_hi, b_lo = split2(b)
        s_hi, s_lo = split2(xw[j, 17:18, :])
        line = iota((16, half), 0)
        bias = jnp.where(line == 0, s_hi.astype(F32), jnp.where(line == 1, s_lo.astype(F32), 0.0))
        return jnp.concatenate([b_hi, b_lo, b_hi, bias.astype(BF16)], 0)

    bk, bv, bq = basis(1), basis(2), basis(0)
    lane = iota((256, PAIR), 1)
    for b in range(full // 256):
        cut = slice(b * 256, (b + 1) * 256)
        ts = tstack[:, cut]
        kk = contract_first(ts, bk)
        vv = contract_first(ts, bv)
        for p in range(npairs):
            k_s[p, cut, :] = kk[:, p * PAIR : (p + 1) * PAIR].astype(BF16)
            vp = vv[:, p * PAIR : (p + 1) * PAIR]
            v_s[2 * p, cut, :] = jnp.where(
                lane < HEAD_DIM, vp, jnp.where(lane < HEAD_DIM + 2, 1.0, 0.0)).astype(BF16)
            v_s[2 * p + 1, cut, :] = jnp.where(
                lane >= HEAD_DIM, vp, jnp.where(lane < 2, 1.0, 0.0)).astype(BF16)
    chip_cut = pl.ds(pl.multiple_of(chip * own, LANES), own)
    qq = contract_first(bq, tstack[:, chip_cut]).astype(BF16) * BF16(HEAD_DIM ** -0.5)
    blank = jnp.zeros((HEAD_DIM, own), BF16)
    for p in range(npairs):
        qt[2 * p] = jnp.concatenate([qq[p * PAIR : p * PAIR + HEAD_DIM], blank], 0)
        qt[2 * p + 1] = jnp.concatenate([blank, qq[p * PAIR + HEAD_DIM : (p + 1) * PAIR]], 0)

    def att_copy(p):
        return remote(att.at[core, p], att.at[core, p], a_send.at[p], a_recv.at[p], partner)

    def forward(p, _):
        for b in range(own // 256):
            cut = slice(b * 256, (b + 1) * 256)
            tops = []
            for h in range(2):
                s = plain(k_s[p], qt[2 * p + h, :, cut])
                e = jnp.exp(s - jnp.max(s, 0, keepdims=True)).astype(BF16)
                e_s[2 * p + h, :, cut] = e
                o = contract_first(v_s[2 * p + h], e)
                at = HEAD_DIM if h == 0 else 0
                r = 1.0 / o[at : at + 1]
                r_s[p, h : h + 1, cut] = r
                tops.append(o[h * HEAD_DIM : (h + 1) * HEAD_DIM] * r)
            o = jnp.concatenate(tops, 0)
            attt[p, :, cut] = o.astype(BF16)
            att[core, p, cut, :] = o.T.astype(BF16)
        att_copy(p).start()
        return 0

    lax.fori_loop(0, npairs, forward, 0)
    dino_copy.wait()
    for p in range(npairs):
        att_copy(p).wait_recv()

    spread[...] = jnp.zeros_like(spread)
    loss_s[...] = jnp.zeros_like(loss_s)
    vs[...] = jnp.zeros_like(vs)
    tstack[0:48, :] = tok3
    ep_parts = jnp.concatenate(split2(ep[...]), 0)

    def middle(b, _):
        line = pl.ds(pl.multiple_of(b * 256, 256), 256)
        piece = pl.ds(pl.multiple_of(chip * own + b * 256, LANES), 256)
        a = jnp.concatenate([att[i, p, line, :] for i in range(2) for p in range(npairs)], 1)
        resid = contract_first(tstack[0:48, piece], emb3) + plain(a, out_w[...])
        rb = resid.astype(BF16)
        residb[line, :] = rb
        zp = plain(rb, proj_w[...])
        d = dino[b].astype(F32)
        norm_p = jnp.sqrt(jnp.sum(zp * zp, -1, keepdims=True) + cosine_eps)
        norm_t = jnp.sqrt(jnp.sum(d * d, -1, keepdims=True) + cosine_eps)
        cos = jnp.sum(zp * d, -1, keepdims=True) / (norm_p * norm_t)
        g = (zp * (cos / (norm_p * norm_p)) - d / (norm_p * norm_t)).astype(BF16)
        gzp[line, :] = g
        loss_s[...] += jnp.sum(1.0 - cos, 0, keepdims=True) * 0.5
        return 0

    lax.fori_loop(0, own // 256, middle, 0)

    rh = residb[:, pl.ds(pl.multiple_of(core * half, LANES), half)]
    gp_part = contract_first(rh, gzp[...]).astype(BF16)
    gp[...] = gp_part.reshape(gp.shape)
    others(chips, my_chip, lambda j: remote(
        gp.at[j], gp_recv.at[my_chip], g_send.at[j], g_recv.at[my_chip], same_core(j)).start())

    gatt = contract_last(mt[...], gzp[...]).astype(BF16)
    yrr = contract_last(ep_parts, gzp[...])
    yr[...] = (yrr[0:f_rows] + yrr[f_rows : 2 * f_rows]) * 0.5
    line16 = iota((16, own), 0)
    for p in range(npairs):
        g = gatt[p * PAIR : (p + 1) * PAIR].astype(F32)
        prod = g * attt[p].astype(F32)
        for h in range(2):
            cut = slice(h * HEAD_DIM, (h + 1) * HEAD_DIM)
            r = r_s[p, h : h + 1, :]
            delta = jnp.sum(prod[cut], 0, keepdims=True) * r
            d_hi, d_lo = split2(-delta)
            gr = (g[cut] * r).astype(BF16)
            extra = jnp.where(
                line16 == 0, d_hi.astype(F32), jnp.where(line16 == 1, d_lo.astype(F32), 0.0))
            fill = jnp.concatenate(
                [extra.astype(BF16), jnp.zeros((HEAD_DIM - 16, own), BF16)], 0)
            gt_aug[2 * p + h] = jnp.concatenate([gr, fill] if h == 0 else [fill, gr], 0)
            gt[2 * p + h] = jnp.concatenate([gr, blank] if h == 0 else [blank, gr], 0)

    def backward(p, _):
        q_pair = jnp.concatenate([qt[2 * p], qt[2 * p + 1]], 1)
        g_pair = jnp.concatenate([gt[2 * p], gt[2 * p + 1]], 1)
        for c in range(full // 256):
            cut = slice(c * 256, (c + 1) * 256)
            dss, es = [], []
            for h in range(2):
                dp = plain(v_s[2 * p + h, cut, :], gt_aug[2 * p + h])
                e = e_s[2 * p + h, cut, :]
                ds = (e.astype(F32) * dp).astype(BF16)
                ds_s[h, cut, :] = ds
                dss.append(ds)
                es.append(e)
            gk_s[p, cut, :] = contract_last(jnp.concatenate(dss, 1), q_pair).astype(BF16)
            gv_s[p, cut, :] = contract_last(jnp.concatenate(es, 1), g_pair).astype(BF16)
        outs = []
        for h in range(2):
            o = contract_first(k_s[p], ds_s[h])
            outs.append(o[h * HEAD_DIM : (h + 1) * HEAD_DIM] * HEAD_DIM ** -0.5)
        gqt[pl.ds(pl.multiple_of(p * PAIR, PAIR), PAIR), :] = jnp.concatenate(outs, 0).astype(BF16)
        return 0

    lax.fori_loop(0, npairs, backward, 0)

    def weights(j):
        return jnp.concatenate(split2(xw[j]), 0)

    inv = inv_s[...]
    tn = tokens[...]
    y = contract_last(weights(1), jnp.concatenate([gk_s[p] for p in range(npairs)], 1))
    y = y + contract_last(weights(2), jnp.concatenate([gv_s[p] for p in range(npairs)], 1))
    y = y[0:24] + y[24:48]
    yq = plain(weights(0), gqt[...])
    yq = yq[0:24] + yq[24:48]

    def back(y, inv, tn, gct):
        yc = y[0:16] - ebar * y[16:17]
        return inv * (yc - gct * jnp.sum(tn * yc, 0, keepdims=True))

    sp = back(y, inv, tn, gct[...])
    sq = back(yq, inv_s[:, chip_cut], tokens[:, chip_cut], gct[:, chip_cut]) + yr[...]
    for t in range(full // LANES):
        spread[t + 1] = sp[:, t * LANES : (t + 1) * LANES]
    for t in range(own // LANES):
        spread[chip * (own // LANES) + t + 1] += sq[:, t * LANES : (t + 1) * LANES]
    strip = block // LANES
    s_copies = []
    for d in range(1, slabs):
        peer = lax.rem(slab + d, slabs)
        s_copies.append(remote(
            spread.at[pl.ds(peer * strip, strip + 2)], spread_all.at[slab],
            s_send.at[d], s_recv.at[d], {"slab": peer, "img": image}))
    for c in s_copies:
        c.start()
    spread_all[slab] = spread[pl.ds(slab * strip, strip + 2)]
    for c in s_copies:
        c.wait_recv()

    cells = []
    for t in range(strip + 2):
        g = spread_all[0, t]
        for p in range(1, slabs):
            g = g + spread_all[p, t]
        g = (g * latent_scale).astype(BF16)
        cells.append(jnp.concatenate([g[0:8], g[8:16]], 1))
    stack[0 : 8 * (strip + 2), :] = contract_last(jnp.concatenate(cells, 0), select)
    for r in range(rows):
        cut = slice(r * LANES, (r + 1) * LANES)
        for ky in range(3):
            h = r + 1 - ky + 4
            t, rest = divmod(h, 4)
            p, dy = divmod(rest, 2)
            vs[16 + ky * 4 : 20 + ky * 4, cut] = stack[
                t * 8 + dy * 4 : t * 8 + dy * 4 + 4, p * LANES : (p + 1) * LANES]
        mid_view = vs[16:32, cut]
        vs[0:16, cut] = shifted(mid_view, -1)
        vs[32:48, cut] = shifted(mid_view, 1)
    views = vs[...].astype(BF16)
    conv_part = plain(views, feats[...])
    cbuf[...] = jnp.zeros_like(cbuf)
    for i in range(TAPS // 8):
        for j in range(4):
            cbuf[i * 4 + j] = conv_part[i * 8 : i * 8 + 8, j * LANES : (j + 1) * LANES]
    cbuf[TAPS // 2] = jnp.broadcast_to(loss_s[...], (8, LANES))
    others(devices, me, lambda j: remote(
        cbuf.at[j], crecv.at[me], c_send.at[j], c_recv.at[me], anyone(j)).start())
    for b in range(rows * LANES // 256):
        cut = slice(b * 256, (b + 1) * 256)
        gfeat_ref[cut, :] = contract_first(views[:, cut], taps48[...]).astype(BF16)

    others(devices, me, lambda j: remote(
        cbuf.at[me], crecv.at[j], c_send.at[j], c_recv.at[j], anyone(j)).wait_recv())
    total = lax.fori_loop(
        1, devices, lambda i, acc: acc + crecv[lax.rem(me + i, devices)], cbuf[me])
    cfull[me] = total
    others(devices, me, lambda j: remote(
        cfull.at[me], cfull.at[me], d_send.at[j], d_recv.at[me], anyone(j)).start())

    others(chips, my_chip, lambda j: remote(
        gp.at[my_chip], gp_recv.at[j], g_send.at[j], g_recv.at[j], same_core(j)).wait_recv())
    gsum = lax.fori_loop(
        1, chips, lambda i, acc: acc + gp_recv[lax.rem(my_chip + i, chips)].astype(F32),
        gp[my_chip].astype(F32))
    gp_out[core, my_chip] = gsum.astype(BF16)
    others(chips, my_chip, lambda j: remote(
        gp_out.at[core, my_chip], gp_out.at[core, my_chip], h_send.at[j], h_recv.at[my_chip],
        same_core(j)).start())
    others(chips, my_chip, lambda j: remote(
        gp_out.at[core, my_chip], gp_out.at[core, j], h_send.at[j], h_recv.at[j],
        same_core(j)).wait_recv())
    last = remote(gp_out.at[core], gp_out.at[core], p_sems.at[0], p_sems.at[1], partner)
    last.start()

    others(devices, me, lambda j: remote(
        cfull.at[me], cfull.at[j], d_send.at[j], d_recv.at[j], anyone(j)).wait_recv())
    for i in range(TAPS // 8):
        for j in range(4):
            vs[i * 8 : i * 8 + 8, j * LANES : (j + 1) * LANES] = cfull[i * 4 + j]
    for kx in range(3):
        for ky in range(3):
            gconv_ref[ky * 3 + kx] = vs[kx * 16 + ky * 4 : kx * 16 + ky * 4 + 4, : 4 * LANES]
    loss_ref[...] = cfull[TAPS // 2, 0:1, 0:1] * (1.0 / (devices * block))
    gproj_ref[core] = gp_out[core].astype(F32).reshape(gproj_ref.shape[1:])
    remote(
        gp_out.at[core], gp_out.at[1 - core], p_sems.at[0], p_sems.at[1], partner).wait_recv()
    gproj_ref[1 - core] = gp_out[1 - core].astype(F32).reshape(gproj_ref.shape[1:])

    for c in t_copies + s_copies + [last]:
        c.wait_send()
    for p in range(npairs):
        att_copy(p).wait_send()
    others(devices, me, lambda j: remote(
        cbuf.at[j], crecv.at[me], c_send.at[j], c_recv.at[me], anyone(j)).wait_send())
    others(devices, me, lambda j: remote(
        cfull.at[me], cfull.at[me], d_send.at[j], d_recv.at[me], anyone(j)).wait_send())
    others(chips, my_chip, lambda j: remote(
        gp.at[j], gp_recv.at[my_chip], g_send.at[j], g_recv.at[my_chip],
        same_core(j)).wait_send())
    others(chips, my_chip, lambda j: remote(
        gp_out.at[core, my_chip], gp_out.at[core, my_chip], h_send.at[j], h_recv.at[my_chip],
        same_core(j)).wait_send())


def local(feats, labels, conv_w, embed_w, mod_table, qkv_w, out_w, proj_w, dino):
    _, rows, cols, chans = feats.shape
    width = qkv_w.shape[0]
    deep = proj_w.shape[1]
    slabs = lax.axis_size("slab")
    images = lax.axis_size("img")
    devices = slabs * images
    chips = devices // 2
    half = width // 2
    block = dino.shape[1]
    own = 2 * block
    full = slabs * block
    heads = half // HEAD_DIM
    pairs = half // PAIR
    features = embed_w.shape[0]
    taps = conv_w.transpose(0, 2, 1)
    row = lax.dynamic_slice_in_dim(mod_table, labels[0], 1, 0).reshape(2, width).astype(F32)
    vmem = pl.BlockSpec(memory_space=pltpu.VMEM)
    hbm = pl.BlockSpec(memory_space=pl.ANY)
    dma = pltpu.SemaphoreType.DMA
    strip = block // LANES
    V = pltpu.VMEM
    scratch = [
        V((rows * cols, chans), BF16), V((3, width, half), BF16), V((width, width), BF16),
        V((width, deep), BF16), V((2, block, deep), BF16), dma((7,)),
        V((TAPS, chans), BF16), V((rows, 16, LANES), F32), V((rows // 2 + 2, 8, LANES), F32),
        V((slabs, rows // 2 + 2, 8, LANES), F32), V((rows * slabs // 4 * 8, 2 * LANES), F32),
        V((features, full), F32), V((features, width), F32), V((3, 24, half), F32),
        V((64, full), BF16), V((half, deep), BF16), V((features, deep), F32),
        V((1, full), F32), V((features, full), F32), V((pairs, full, PAIR), BF16),
        V((heads, full, PAIR), BF16), V((heads, PAIR, own), BF16), V((heads, full, own), BF16),
        V((pairs, 2, own), F32), V((pairs, PAIR, own), BF16), V((2, pairs, own, PAIR), BF16),
        V((own, width), BF16), V((own, deep), BF16), V((heads, PAIR, own), BF16),
        V((heads, PAIR, own), BF16), V((2, full, own), BF16),
        V((pairs, full, PAIR), BF16), V((pairs, full, PAIR), BF16), V((half, own), BF16),
        V((features, own), F32), V((full // LANES + 2, features, LANES), F32),
        V((slabs, strip + 2, features, LANES), F32), V((TAPS, rows * cols), F32),
        V((devices, 8, LANES), F32), V((devices, 8, LANES), F32), V((devices, 8, LANES), F32),
        V((chips, half // chips, deep), BF16), V((chips, half // chips, deep), BF16),
        V((2, chips, half // chips, deep), BF16), V((1, 1), F32),
        dma((2,)), dma((slabs,)), dma((slabs,)), dma((pairs,)), dma((pairs,)),
        dma((slabs,)), dma((slabs,)), dma((devices,)), dma((devices,)), dma((devices,)),
        dma((devices,)), dma((chips,)), dma((chips,)), dma((chips,)), dma((chips,)), dma((2,)),
    ]
    gfeat, gproj, gconv, loss = pl.pallas_call(
        functools.partial(step_kernel, slabs, images),
        out_shape=[
            jax.ShapeDtypeStruct((rows * cols, chans), BF16),
            jax.ShapeDtypeStruct((2, half, deep), F32),
            jax.ShapeDtypeStruct((9, conv_w.shape[2], chans), F32),
            jax.ShapeDtypeStruct((1, 1), F32),
        ],
        in_specs=[hbm, vmem, vmem, vmem, hbm, hbm, hbm, hbm],
        out_specs=[vmem] * 4,
        scratch_shapes=scratch,
        compiler_params=pltpu.CompilerParams(
            collective_id=0, has_side_effects=True, vmem_limit_bytes=60 * 1024 * 1024),
        name="step",
    )(feats.reshape(rows * cols, chans), taps, embed_w, row, qkv_w, out_w, proj_w, dino[0])
    return (
        gfeat.reshape(feats.shape), gproj.reshape(width, deep), gconv.transpose(0, 2, 1),
        loss.reshape(()),
    )


def solution(mesh):
    in_specs = (
        P("img", "slab", None, None),
        P("img"),
        P(),
        P(),
        P(),
        P(),
        P(),
        P(),
        P("img", "slab", None),
    )
    out_specs = (P("img", "slab", None, None), P(), P(), P())
    return jax.shard_map(local, mesh=mesh, in_specs=in_specs, out_specs=out_specs, check_vma=False)
```

time: 165 us -> 92.4 us (0.56)
  matrix products: 41 us -> 0 us
  blocking collectives: 12.8 us -> 0 us
  other arithmetic: 11.8 us -> 0.79 us
  local copies, waits for them, and re-layouts: 14.7 us -> 7.29 us
    dot_general x16 -> x0, matrix products: 41 us -> none  [the longest x11 24.6 us: mm(): lax.dot_general(left, right, (dims, ((), ())), preferred_element_type=kind)]
    all_gather x2 -> x0, blocking collectives: 12.8 us -> none  [the longest x1 6.51 us: local(): terms_all = lax.all_gather(terms, 'slab', axis=0)]
    convert_element_type x5 -> x1, other arithmetic: 9.17 us -> 0.79 us  [local(): lax.dynamic_slice_in_dim(mod_table, labels[0], 1, 0).reshape(2, width)]
    unnamed x31 -> x5, local copies, waits for them, and re-layouts: 3.28 us -> 6.69 us
    transpose x2 -> x0, local copies, waits for them, and re-layouts: 3.4 us -> none  [the longest x1 2.77 us: local(): latent.reshape(outs, full_rows // 2, 2, cols // 2, 2)]
    convert_element_type x3 -> x1, local copies, waits for them, and re-layouts: 3.85 us -> 0.61 us  [local(): lax.dynamic_slice_in_dim(mod_table, labels[0], 1, 0).reshape(2, width)]
    mul x1 -> x0, local copies, waits for them, and re-layouts: 1.97 us -> none  [local(): sum((jnp.pad(terms_all[s], ((0, 0), (s * rows, full_rows - (s + 1) * rows...]
    pallas_call x3 -> x1, Pallas kernels: 81 us -> 80.5 us  [local(): pl.pallas_call(functools.partial(step_kernel, slabs, images), out_shape=[...]
where the time goes in v1:
time: 92.4 us; the launch traced here: 91.7 us
  Pallas kernels  80.5 us (87%)
  local copies, waits for them, and re-layouts  7.29 us (8%)
  between operations  3.1 us (3%)
    pallas_call x1, Pallas kernels, local(): pl.pallas_call(functools.partial(step_kernel, slabs, images), out_shape=[...  80.5 us
    unnamed x5, local copies, waits for them, and re-layouts  6.69 us

profile of v1, /device:TPU:0, one launch (start us, length us, event | category | flops | bytes accessed | tf_op | source)
XLA Modules:
  0.0 91.7 jit_solution(13197753885876562000)
XLA Ops:
  1.3 0.8 convert_reduce_fusion
  2.1 0.6 reshape.27.row_ref
  2.7 80.5 %step.1 = (bf16[1024,512]{1,0:T(8,128)(2,1)}, f32[2,512,768]{2,1,0:T(8,128)}, f32[9,4,512]{2,1,0:T(4,128)}, f32[1,1]{1,0:T(1,128)}) custom-call(bf16[1024,512]{1,0:T(8,128)(2,1)} %bitcast.12, bf16[9,4,512]{2,1,0:T(4,128)(2,1)} %bitcast.16, bf16[16,1024]{1,0:T(8,128)(2,1)} %embed_ref.1, f32[2,1024]{1,0:T(2,128)} %reshape.27.row_ref, ...), custom_call_target="tpu_custom_call" | custom-call | tf_op jit(solution)/shard_map/step/pallas_call | solution.py:528
  83.2 2.3 %copy.18 = bf16[1,8,128,512]{3,2,1,0:T(8,128)(2,1)} copy(bf16[1,8,128,512]{3,2,1,0:T(8,128)(2,1)} %bitcast.13) | data formatting | bytes 2097152
  85.4 0.0 copy-start
  85.4 3.8 %copy.19 = f32[1024,768]{1,0:T(8,128)} copy(f32[1024,768]{1,0:T(8,128)} %bitcast.11) | data formatting | bytes 6291456
  89.2 0.0 copy-done
  89.2 0.6 copy.20
Async XLA Ops:
  85.4 3.8 %copy-start = (f32[9,4,512]{2,1,0:T(4,128)S(1)}, f32[9,4,512]{2,1,0:T(4,128)}, u32[]{:S(2)}) copy-start(f32[9,4,512]{2,1,0:T(4,128)} %get-tuple-element.10) | copy-start | bytes 221188

commit v2 on v1

--- a/solution.py
+++ b/solution.py
@@ -11,6 +11,7 @@
 PAIR = 2 * HEAD_DIM
 LANES = 128
 TAPS = 48
+GRANT = 60 * 1024 * 1024
 
 latent_scale = 0.18215
 norm_eps = 1e-06
@@ -62,15 +63,16 @@
 
 def step_kernel(
     slabs, images,
-    feats_hbm, taps_ref, embed_ref, row_ref, qkv_hbm, out_hbm, proj_hbm, dino_hbm,
-    gfeat_ref, gproj_ref, gconv_ref, loss_ref,
-    feats, w_own, out_w, proj_w, dino, load_sems,
+    feats_hbm, taps_hbm, embed_hbm, row_hbm, qkv_hbm, out_hbm, proj_hbm, dino_hbm,
+    views_hbm, tapsb_hbm, gp_hbm, gconv_hbm, loss_hbm,
+    feats, taps_s, embed_s, row_s, w_own, out_w, proj_w, dino, load_sems,
     taps48, resp_g, terms, terms_all, stack, tokens, emb, xw, tstack, mt, ep,
-    inv_s, gct, k_s, v_s, qt, e_s, r_s, attt, att, residb, gzp, gt_aug, gt, ds_s,
+    inv_s, gct, k_s, v_s, qt, s_s, e_s, r_s, attt, att, residb, gzp, gt_aug, gt, ds_s,
     gk_s, gv_s, gqt, yr, spread, spread_all, vs,
-    cbuf, crecv, cfull, gp, gp_recv, gp_out, loss_s,
+    cbuf, crecv, cfull, gp, r1, h1, r2, h2, r3, gpo, views_s, gconv_s, loss_s, save_sems, gp_sems,
     dino_sems, t_send, t_recv, a_send, a_recv, s_send, s_recv,
-    c_send, c_recv, d_send, d_recv, g_send, g_recv, h_send, h_recv, p_sems,
+    c_send, c_recv, d_send, d_recv, p1_sems, p2_sems, p3_send, p3_recv, a3_send, a3_recv,
+    a2_sems, a1_sems, a0_sems,
 ):
     slab = lax.axis_index("slab")
     image = lax.axis_index("img")
@@ -78,9 +80,13 @@
     chip = slab // 2
     partner = {"slab": slab + 1 - 2 * core, "img": image}
     devices = slabs * images
-    chips = devices // 2
     me = slab * images + image
-    my_chip = chip * images + image
+    depth = images // 2
+    east, north = lax.rem(image, 2), image // 2
+    first = chip + core * (east - chip)
+    second = east + core * (chip - east)
+    hop1 = {"slab": slab + (1 - core) * (2 - 4 * chip), "img": image + core * (1 - 2 * east)}
+    hop2 = {"slab": slab + core * (2 - 4 * chip), "img": image + (1 - core) * (1 - 2 * east)}
     width = out_w.shape[0]
     half = width // 2
     full = tokens.shape[1]
@@ -92,8 +98,8 @@
     def anyone(j):
         return {"slab": j // images, "img": lax.rem(j, images)}
 
-    def same_core(j):
-        return {"slab": (j // images) * 2 + core, "img": lax.rem(j, images)}
+    def level(j):
+        return {"slab": slab, "img": j * 2 + east}
 
     def remote(src, dst, send, recv, device):
         return pltpu.make_async_remote_copy(
@@ -107,31 +113,43 @@
 
         lax.fori_loop(1, count, run, 0)
 
+    barrier = pltpu.get_barrier_semaphore()
     loads = [pltpu.make_async_copy(feats_hbm, feats, load_sems.at[0])]
     for j in range(3):
         loads.append(pltpu.make_async_copy(
             qkv_hbm.at[:, pl.ds(pl.multiple_of(j * width + core * half, LANES), half)],
             w_own.at[j], load_sems.at[1 + j]))
     loads.append(pltpu.make_async_copy(proj_hbm, proj_w, load_sems.at[4]))
-    loads.append(pltpu.make_async_copy(out_hbm, out_w, load_sems.at[5]))
+    loads.append(pltpu.make_async_copy(
+        out_hbm.at[pl.ds(pl.multiple_of(core * half, 8), half)],
+        out_w.at[pl.ds(pl.multiple_of(core * half, 8), half)], load_sems.at[5]))
     loads.append(pltpu.make_async_copy(dino_hbm, dino.at[core], load_sems.at[6]))
-    for c in loads:
-        c.start()
-
-    barrier = pltpu.get_barrier_semaphore()
+    loads.append(pltpu.make_async_copy(taps_hbm, taps_s, load_sems.at[7]))
+    loads.append(pltpu.make_async_copy(embed_hbm, embed_s, load_sems.at[8]))
+    loads.append(pltpu.make_async_copy(row_hbm, row_s, load_sems.at[9]))
+    loads.append(pltpu.make_async_copy(
+        out_hbm.at[pl.ds(pl.multiple_of((1 - core) * half, 8), half)],
+        out_w.at[pl.ds(pl.multiple_of((1 - core) * half, 8), half)], load_sems.at[10]))
+    for i in (7, 8, 0, 9, 4, 5, 1, 2, 3, 6, 10):
+        loads[i].start()
+
     others(devices, me, lambda j: pl.semaphore_signal(
         barrier, inc=1, device_id=anyone(j), device_id_type=MESH_ID))
 
     vs[...] = jnp.zeros_like(vs)
+    loads[7].wait()
+    loads[8].wait()
     for kx in range(3):
         for ky in range(3):
             vs[kx * 16 + ky * 4 : kx * 16 + ky * 4 + 4, : feats.shape[1]] = (
-                taps_ref[ky * 3 + kx].astype(F32))
+                taps_s[ky * 3 + kx].astype(F32))
     taps48[...] = vs[:, : feats.shape[1]].astype(BF16)
+    saves = [pltpu.make_async_copy(taps48, tapsb_hbm, save_sems.at[0])]
+    saves[0].start()
     for dy in range(2):
         for dx in range(2):
             emb[dx * 8 + dy * 4 : dx * 8 + dy * 4 + 4, :] = (
-                embed_ref[dy * 8 + dx * 4 : dy * 8 + dx * 4 + 4, :].astype(F32))
+                embed_s[dy * 8 + dx * 4 : dy * 8 + dx * 4 + 4, :].astype(F32))
 
     loads[0].wait()
     resp = contract_last(taps48[...], feats[...])
@@ -166,24 +184,26 @@
     dino_copy.start()
     terms_all[slab] = terms[...]
 
-    gain = 1.0 + row_ref[1:2, :]
+    loads[4].wait()
+    ep[...] = plain(emb[...].astype(BF16), proj_w[...])
+    loads[5].wait()
+    mt[...] = plain(
+        out_w[pl.ds(pl.multiple_of(core * half, 8), half), :], proj_w[...]).astype(BF16)
+    ebar = jnp.mean(emb[...], 1, keepdims=True)
+    ecent = emb[...] - ebar
+    gram = lax.dot_general(
+        ecent, ecent, (((1,), (1,)), ((), ())), precision=lax.Precision.HIGHEST,
+        preferred_element_type=F32)
+    loads[9].wait()
+    row = row_s[...].astype(F32)
+    gain = 1.0 + row[:, width:]
     stack_l = jnp.concatenate(
-        [emb[...] * gain, gain, row_ref[0:1, :], jnp.zeros((6, width), F32)], 0)
+        [emb[...] * gain, gain, row[:, :width], jnp.zeros((6, width), F32)], 0)
     parts = jnp.concatenate(split3(stack_l), 0)
     for j in range(3):
         loads[1 + j].wait()
         prod = plain(parts, w_own[j])
         xw[j] = prod[0:24] + prod[24:48] + prod[48:72]
-    ebar = jnp.mean(emb[...], 1, keepdims=True)
-    ecent = emb[...] - ebar
-    gram = lax.dot_general(
-        ecent, ecent, (((1,), (1,)), ((), ())), precision=lax.Precision.HIGHEST,
-        preferred_element_type=F32)
-    loads[4].wait()
-    ep[...] = plain(emb[...].astype(BF16), proj_w[...])
-    loads[5].wait()
-    mt[...] = plain(
-        out_w[pl.ds(pl.multiple_of(core * half, 8), half), :], proj_w[...]).astype(BF16)
 
     for c in t_copies:
         c.wait_recv()
@@ -263,26 +283,42 @@
     def att_copy(p):
         return remote(att.at[core, p], att.at[core, p], a_send.at[p], a_recv.at[p], partner)
 
-    def forward(p, _):
-        for b in range(own // 256):
-            cut = slice(b * 256, (b + 1) * 256)
-            tops = []
-            for h in range(2):
-                s = plain(k_s[p], qt[2 * p + h, :, cut])
-                e = jnp.exp(s - jnp.max(s, 0, keepdims=True)).astype(BF16)
-                e_s[2 * p + h, :, cut] = e
-                o = contract_first(v_s[2 * p + h], e)
-                at = HEAD_DIM if h == 0 else 0
-                r = 1.0 / o[at : at + 1]
-                r_s[p, h : h + 1, cut] = r
-                tops.append(o[h * HEAD_DIM : (h + 1) * HEAD_DIM] * r)
-            o = jnp.concatenate(tops, 0)
-            attt[p, :, cut] = o.astype(BF16)
-            att[core, p, cut, :] = o.T.astype(BF16)
-        att_copy(p).start()
-        return 0
-
-    lax.fori_loop(0, npairs, forward, 0)
+    units = [(p, b, h) for p in range(npairs) for b in range(own // 256) for h in range(2)]
+
+    def scores(i):
+        p, b, h = units[i]
+        s = plain(k_s[p], qt[2 * p + h, :, b * 256 : (b + 1) * 256])
+        s_s[i % 3] = s
+        return jnp.max(s, 0, keepdims=True)
+
+    def weigh(i, top):
+        p, b, h = units[i]
+        e_s[2 * p + h, :, b * 256 : (b + 1) * 256] = jnp.exp(s_s[i % 3] - top).astype(BF16)
+
+    def gather(i, kept):
+        p, b, h = units[i]
+        cut = slice(b * 256, (b + 1) * 256)
+        o = contract_first(v_s[2 * p + h], e_s[2 * p + h, :, cut])
+        at = HEAD_DIM if h == 0 else 0
+        r = 1.0 / o[at : at + 1]
+        r_s[p, h : h + 1, cut] = r
+        kept[h] = o[h * HEAD_DIM : (h + 1) * HEAD_DIM] * r
+        if h == 1:
+            both = jnp.concatenate(kept, 0)
+            attt[p, :, cut] = both.astype(BF16)
+            att[core, p, cut, :] = both.T.astype(BF16)
+            if b == own // 256 - 1:
+                att_copy(p).start()
+
+    kept, top = [None, None], scores(0)
+    for i in range(len(units) + 1):
+        later = scores(i + 1) if i + 1 < len(units) else None
+        if i < len(units):
+            weigh(i, top)
+        if i > 0:
+            gather(i - 1, kept)
+        top = later
+    loads[10].wait()
     dino_copy.wait()
     for p in range(npairs):
         att_copy(p).wait_recv()
@@ -313,10 +349,71 @@
     lax.fori_loop(0, own // 256, middle, 0)
 
     rh = residb[:, pl.ds(pl.multiple_of(core * half, LANES), half)]
-    gp_part = contract_first(rh, gzp[...]).astype(BF16)
-    gp[...] = gp_part.reshape(gp.shape)
-    others(chips, my_chip, lambda j: remote(
-        gp.at[j], gp_recv.at[my_chip], g_send.at[j], g_recv.at[my_chip], same_core(j)).start())
+    chunks, wide = gp.shape[0], gp.shape[-1]
+    ranks = range(chunks)
+
+    def p1(k):
+        return remote(gp.at[k, 1 - first], r1.at[k], p1_sems.at[0, k], p1_sems.at[1, k], hop1)
+
+    def p2(k):
+        return remote(h1.at[k, 1 - second], r2.at[k], p2_sems.at[0, k], p2_sems.at[1, k], hop2)
+
+    def p3(k, j, slot, sem):
+        return remote(h2.at[k, j], r3.at[k, slot], p3_send.at[k, j], p3_recv.at[k, sem], level(j))
+
+    def a3(k, j, slot):
+        return remote(
+            gpo.at[core, k, first, second, north], gpo.at[core, k, first, second, slot],
+            a3_send.at[k, j], a3_recv.at[k, slot], level(j))
+
+    def a2(k, there):
+        return remote(
+            gpo.at[core, k, first, second], gpo.at[core, k, first, there],
+            a2_sems.at[0, k], a2_sems.at[1, k], hop2)
+
+    def a1(k, there):
+        return remote(
+            gpo.at[core, k, first], gpo.at[core, k, there],
+            a1_sems.at[0, k], a1_sems.at[1, k], hop1)
+
+    def a0(k, there):
+        return remote(
+            gpo.at[core, k], gpo.at[there, k], a0_sems.at[0, k], a0_sems.at[1, k], partner)
+
+    def add1(k):
+        p1(k).wait_recv()
+        h1[k] = (gp[k, first].astype(F32) + r1[k].astype(F32)).astype(BF16)
+        p2(k).start()
+
+    def add2(k):
+        p2(k).wait_recv()
+        h2[k] = (h1[k, second].astype(F32) + r2[k].astype(F32)).astype(BF16)
+        others(depth, north, lambda j: p3(k, j, north, north).start())
+
+    def add3(k):
+        others(depth, north, lambda j: p3(k, j, j, j).wait_recv())
+        total = lax.fori_loop(
+            1, depth, lambda i, acc: acc + r3[k, lax.rem(north + i, depth)].astype(F32),
+            h2[k, north].astype(F32))
+        gpo[core, k, first, second, north] = total.astype(BF16)
+        others(depth, north, lambda j: a3(k, j, north).start())
+
+    def give3(k):
+        others(depth, north, lambda j: a3(k, j, j).wait_recv())
+        a2(k, second).start()
+
+    def give2(k):
+        a2(k, 1 - second).wait_recv()
+        a1(k, first).start()
+
+    def give1(k):
+        a1(k, 1 - first).wait_recv()
+        a0(k, core).start()
+
+    for k in ranks:
+        part = contract_first(rh, gzp[:, k * wide : (k + 1) * wide]).astype(BF16)
+        gp[k] = part.reshape(gp.shape[1:])
+        p1(k).start()
 
     gatt = contract_last(mt[...], gzp[...]).astype(BF16)
     yrr = contract_last(ep_parts, gzp[...])
@@ -358,10 +455,13 @@
             o = contract_first(k_s[p], ds_s[h])
             outs.append(o[h * HEAD_DIM : (h + 1) * HEAD_DIM] * HEAD_DIM ** -0.5)
         gqt[pl.ds(pl.multiple_of(p * PAIR, PAIR), PAIR), :] = jnp.concatenate(outs, 0).astype(BF16)
+        for k in ranks:
+            pl.when(p == min(k + 1, npairs - 1))(functools.partial(add1, k))
         return 0
 
     lax.fori_loop(0, npairs, backward, 0)
 
+    add2(0)
     def weights(j):
         return jnp.concatenate(split2(xw[j]), 0)
 
@@ -393,6 +493,8 @@
     for c in s_copies:
         c.start()
     spread_all[slab] = spread[pl.ds(slab * strip, strip + 2)]
+    for k in ranks[1:]:
+        add2(k)
     for c in s_copies:
         c.wait_recv()
 
@@ -416,6 +518,9 @@
         vs[0:16, cut] = shifted(mid_view, -1)
         vs[32:48, cut] = shifted(mid_view, 1)
     views = vs[...].astype(BF16)
+    views_s[...] = views
+    saves.append(pltpu.make_async_copy(views_s, views_hbm, save_sems.at[1]))
+    saves[-1].start()
     conv_part = plain(views, feats[...])
     cbuf[...] = jnp.zeros_like(cbuf)
     for i in range(TAPS // 8):
@@ -424,10 +529,9 @@
     cbuf[TAPS // 2] = jnp.broadcast_to(loss_s[...], (8, LANES))
     others(devices, me, lambda j: remote(
         cbuf.at[j], crecv.at[me], c_send.at[j], c_recv.at[me], anyone(j)).start())
-    for b in range(rows * LANES // 256):
-        cut = slice(b * 256, (b + 1) * 256)
-        gfeat_ref[cut, :] = contract_first(views[:, cut], taps48[...]).astype(BF16)
-
+    for k in ranks:
+        add3(k)
+    give3(0)
     others(devices, me, lambda j: remote(
         cbuf.at[me], crecv.at[j], c_send.at[j], c_recv.at[j], anyone(j)).wait_recv())
     total = lax.fori_loop(
@@ -436,21 +540,10 @@
     others(devices, me, lambda j: remote(
         cfull.at[me], cfull.at[me], d_send.at[j], d_recv.at[me], anyone(j)).start())
 
-    others(chips, my_chip, lambda j: remote(
-        gp.at[my_chip], gp_recv.at[j], g_send.at[j], g_recv.at[j], same_core(j)).wait_recv())
-    gsum = lax.fori_loop(
-        1, chips, lambda i, acc: acc + gp_recv[lax.rem(my_chip + i, chips)].astype(F32),
-        gp[my_chip].astype(F32))
-    gp_out[core, my_chip] = gsum.astype(BF16)
-    others(chips, my_chip, lambda j: remote(
-        gp_out.at[core, my_chip], gp_out.at[core, my_chip], h_send.at[j], h_recv.at[my_chip],
-        same_core(j)).start())
-    others(chips, my_chip, lambda j: remote(
-        gp_out.at[core, my_chip], gp_out.at[core, j], h_send.at[j], h_recv.at[j],
-        same_core(j)).wait_recv())
-    last = remote(gp_out.at[core], gp_out.at[core], p_sems.at[0], p_sems.at[1], partner)
-    last.start()
-
+    for k in ranks[1:]:
+        give3(k)
+    for k in ranks:
+        give2(k)
     others(devices, me, lambda j: remote(
         cfull.at[me], cfull.at[j], d_send.at[j], d_recv.at[j], anyone(j)).wait_recv())
     for i in range(TAPS // 8):
@@ -458,14 +551,26 @@
             vs[i * 8 : i * 8 + 8, j * LANES : (j + 1) * LANES] = cfull[i * 4 + j]
     for kx in range(3):
         for ky in range(3):
-            gconv_ref[ky * 3 + kx] = vs[kx * 16 + ky * 4 : kx * 16 + ky * 4 + 4, : 4 * LANES]
-    loss_ref[...] = cfull[TAPS // 2, 0:1, 0:1] * (1.0 / (devices * block))
-    gproj_ref[core] = gp_out[core].astype(F32).reshape(gproj_ref.shape[1:])
-    remote(
-        gp_out.at[core], gp_out.at[1 - core], p_sems.at[0], p_sems.at[1], partner).wait_recv()
-    gproj_ref[1 - core] = gp_out[1 - core].astype(F32).reshape(gproj_ref.shape[1:])
-
-    for c in t_copies + s_copies + [last]:
+            gconv_s[ky * 3 + kx] = vs[kx * 16 + ky * 4 : kx * 16 + ky * 4 + 4, : 4 * LANES]
+    loss_s[...] = cfull[TAPS // 2, 0:1, 0:1] * (1.0 / (devices * block))
+    saves.append(pltpu.make_async_copy(gconv_s, gconv_hbm, save_sems.at[2]))
+    saves.append(pltpu.make_async_copy(loss_s, loss_hbm, save_sems.at[3]))
+    for c in saves[-2:]:
+        c.start()
+    for k in ranks:
+        give1(k)
+        saves.append(pltpu.make_async_copy(
+            gpo.at[core, k], gp_hbm.at[core, k], gp_sems.at[0, k]))
+        saves[-1].start()
+    for k in ranks:
+        a0(k, 1 - core).wait_recv()
+        saves.append(pltpu.make_async_copy(
+            gpo.at[1 - core, k], gp_hbm.at[1 - core, k], gp_sems.at[1, k]))
+        saves[-1].start()
+    for c in saves:
+        c.wait()
+
+    for c in t_copies + s_copies:
         c.wait_send()
     for p in range(npairs):
         att_copy(p).wait_send()
@@ -473,12 +578,64 @@
         cbuf.at[j], crecv.at[me], c_send.at[j], c_recv.at[me], anyone(j)).wait_send())
     others(devices, me, lambda j: remote(
         cfull.at[me], cfull.at[me], d_send.at[j], d_recv.at[me], anyone(j)).wait_send())
-    others(chips, my_chip, lambda j: remote(
-        gp.at[j], gp_recv.at[my_chip], g_send.at[j], g_recv.at[my_chip],
-        same_core(j)).wait_send())
-    others(chips, my_chip, lambda j: remote(
-        gp_out.at[core, my_chip], gp_out.at[core, my_chip], h_send.at[j], h_recv.at[my_chip],
-        same_core(j)).wait_send())
+    for k in ranks:
+        p1(k).wait_send()
+        p2(k).wait_send()
+        others(depth, north, lambda j, k=k: p3(k, j, north, north).wait_send())
+        others(depth, north, lambda j, k=k: a3(k, j, north).wait_send())
+        a2(k, second).wait_send()
+        a1(k, first).wait_send()
+        a0(k, core).wait_send()
+
+
+def finish_kernel(
+    views_hbm, taps_hbm, gp_hbm, conv_hbm, sum_hbm, gfeat_hbm, gproj_hbm, gconv_hbm, loss_hbm,
+    views, taps, gp, gfeat, gproj, gconv, loss,
+    load_sems, gp_sems, sems,
+):
+    cores, chunks, many, deep, wide = gp.shape
+    loads = [
+        pltpu.make_async_copy(views_hbm, views, load_sems.at[0]),
+        pltpu.make_async_copy(taps_hbm, taps, load_sems.at[1]),
+    ]
+    parts = [
+        pltpu.make_async_copy(gp_hbm.at[i, k], gp.at[i, k], gp_sems.at[i, k])
+        for i in range(cores) for k in range(chunks)]
+    small = [
+        pltpu.make_async_copy(conv_hbm, gconv, load_sems.at[2]),
+        pltpu.make_async_copy(sum_hbm, loss, load_sems.at[3]),
+    ]
+    for c in loads + small + parts:
+        c.start()
+    for c in loads + small:
+        c.wait()
+    copies = [
+        pltpu.make_async_copy(gconv, gconv_hbm, load_sems.at[4]),
+        pltpu.make_async_copy(loss, loss_hbm, load_sems.at[5]),
+    ]
+    for c in copies:
+        c.start()
+    lines = gfeat.shape[1]
+    for i in range(gfeat.shape[0]):
+        gfeat[i] = contract_first(
+            views[:, i * lines : (i + 1) * lines], taps[...]).astype(BF16)
+        copies.append(pltpu.make_async_copy(
+            gfeat.at[i], gfeat_hbm.at[pl.ds(i * lines, lines)], sems.at[0, i]))
+        copies[-1].start()
+    blocks = gproj.shape[0] // cores
+    each = many // blocks
+    lines = each * deep
+    for i in range(cores * blocks):
+        for k in range(chunks):
+            if i % blocks == 0:
+                parts[i // blocks * chunks + k].wait()
+            cut = gp[i // blocks, k, i % blocks * each : (i % blocks + 1) * each]
+            gproj[i, :, k * wide : (k + 1) * wide] = cut.astype(F32).reshape(lines, wide)
+        copies.append(pltpu.make_async_copy(
+            gproj.at[i], gproj_hbm.at[pl.ds(i * lines, lines)], sems.at[1, i]))
+        copies[-1].start()
+    for c in copies:
+        c.wait()
 
 
 def local(feats, labels, conv_w, embed_w, mod_table, qkv_w, out_w, proj_w, dino):
@@ -488,7 +645,6 @@
     slabs = lax.axis_size("slab")
     images = lax.axis_size("img")
     devices = slabs * images
-    chips = devices // 2
     half = width // 2
     block = dino.shape[1]
     own = 2 * block
@@ -497,21 +653,26 @@
     pairs = half // PAIR
     features = embed_w.shape[0]
     taps = conv_w.transpose(0, 2, 1)
-    row = lax.dynamic_slice_in_dim(mod_table, labels[0], 1, 0).reshape(2, width).astype(F32)
-    vmem = pl.BlockSpec(memory_space=pltpu.VMEM)
-    hbm = pl.BlockSpec(memory_space=pl.ANY)
+    row = lax.dynamic_slice_in_dim(mod_table, labels[0], 1, 0)
+    depth = images // 2
+    wide = 2 * LANES
+    piece = half // (4 * depth)
+    chunks = deep // wide
+    hbm = pl.BlockSpec(memory_space=pltpu.HBM)
     dma = pltpu.SemaphoreType.DMA
     strip = block // LANES
     V = pltpu.VMEM
     scratch = [
-        V((rows * cols, chans), BF16), V((3, width, half), BF16), V((width, width), BF16),
-        V((width, deep), BF16), V((2, block, deep), BF16), dma((7,)),
+        V((rows * cols, chans), BF16), V(taps.shape, BF16), V(embed_w.shape, BF16),
+        V((1, 2 * width), BF16), V((3, width, half), BF16), V((width, width), BF16),
+        V((width, deep), BF16), V((2, block, deep), BF16), dma((11,)),
         V((TAPS, chans), BF16), V((rows, 16, LANES), F32), V((rows // 2 + 2, 8, LANES), F32),
         V((slabs, rows // 2 + 2, 8, LANES), F32), V((rows * slabs // 4 * 8, 2 * LANES), F32),
         V((features, full), F32), V((features, width), F32), V((3, 24, half), F32),
         V((64, full), BF16), V((half, deep), BF16), V((features, deep), F32),
         V((1, full), F32), V((features, full), F32), V((pairs, full, PAIR), BF16),
-        V((heads, full, PAIR), BF16), V((heads, PAIR, own), BF16), V((heads, full, own), BF16),
+        V((heads, full, PAIR), BF16), V((heads, PAIR, own), BF16), V((3, full, 256), F32),
+        V((heads, full, own), BF16),
         V((pairs, 2, own), F32), V((pairs, PAIR, own), BF16), V((2, pairs, own, PAIR), BF16),
         V((own, width), BF16), V((own, deep), BF16), V((heads, PAIR, own), BF16),
         V((heads, PAIR, own), BF16), V((2, full, own), BF16),
@@ -519,27 +680,54 @@
         V((features, own), F32), V((full // LANES + 2, features, LANES), F32),
         V((slabs, strip + 2, features, LANES), F32), V((TAPS, rows * cols), F32),
         V((devices, 8, LANES), F32), V((devices, 8, LANES), F32), V((devices, 8, LANES), F32),
-        V((chips, half // chips, deep), BF16), V((chips, half // chips, deep), BF16),
-        V((2, chips, half // chips, deep), BF16), V((1, 1), F32),
+        V((chunks, 2, 2, depth, piece, wide), BF16), V((chunks, 2, depth, piece, wide), BF16),
+        V((chunks, 2, depth, piece, wide), BF16), V((chunks, depth, piece, wide), BF16),
+        V((chunks, depth, piece, wide), BF16), V((chunks, depth, piece, wide), BF16),
+        V((2, chunks, 2, 2, depth, piece, wide), BF16), V((TAPS, rows * cols), BF16),
+        V((9, conv_w.shape[2], chans), F32), V((1, 1), F32), dma((4,)), dma((2, chunks)),
         dma((2,)), dma((slabs,)), dma((slabs,)), dma((pairs,)), dma((pairs,)),
         dma((slabs,)), dma((slabs,)), dma((devices,)), dma((devices,)), dma((devices,)),
-        dma((devices,)), dma((chips,)), dma((chips,)), dma((chips,)), dma((chips,)), dma((2,)),
+        dma((devices,)), dma((2, chunks)), dma((2, chunks)), dma((chunks, depth)),
+        dma((chunks, depth)), dma((chunks, depth)), dma((chunks, depth)), dma((2, chunks)),
+        dma((2, chunks)), dma((2, chunks)),
     ]
-    gfeat, gproj, gconv, loss = pl.pallas_call(
+    views, tapsb, gp, conv, total = pl.pallas_call(
         functools.partial(step_kernel, slabs, images),
         out_shape=[
-            jax.ShapeDtypeStruct((rows * cols, chans), BF16),
-            jax.ShapeDtypeStruct((2, half, deep), F32),
+            jax.ShapeDtypeStruct((TAPS, rows * cols), BF16),
+            jax.ShapeDtypeStruct((TAPS, chans), BF16),
+            jax.ShapeDtypeStruct((2, chunks, 2, 2, depth, piece, wide), BF16),
             jax.ShapeDtypeStruct((9, conv_w.shape[2], chans), F32),
             jax.ShapeDtypeStruct((1, 1), F32),
         ],
-        in_specs=[hbm, vmem, vmem, vmem, hbm, hbm, hbm, hbm],
-        out_specs=[vmem] * 4,
+        in_specs=[hbm] * 8,
+        out_specs=[hbm] * 5,
         scratch_shapes=scratch,
         compiler_params=pltpu.CompilerParams(
-            collective_id=0, has_side_effects=True, vmem_limit_bytes=60 * 1024 * 1024),
+            collective_id=0, has_side_effects=True, vmem_limit_bytes=GRANT),
         name="step",
-    )(feats.reshape(rows * cols, chans), taps, embed_w, row, qkv_w, out_w, proj_w, dino[0])
+    )(feats.reshape(rows * cols, chans), taps, embed_w, row, qkv_w, out_w, proj_w,
+      dino[0])
+    steps = 4
+    gfeat, gproj, gconv, loss = pl.pallas_call(
+        finish_kernel,
+        in_specs=[hbm] * 5,
+        out_specs=[hbm] * 4,
+        out_shape=[
+            jax.ShapeDtypeStruct((rows * cols, chans), BF16),
+            jax.ShapeDtypeStruct((width, deep), F32),
+            jax.ShapeDtypeStruct(conv.shape, F32),
+            jax.ShapeDtypeStruct((1, 1), F32),
+        ],
+        scratch_shapes=[
+            V((TAPS, rows * cols), BF16), V((TAPS, chans), BF16),
+            V((2, chunks, 4 * depth, piece, wide), BF16),
+            V((steps, rows * cols // steps, chans), BF16), V((steps, width // steps, deep), F32),
+            V(conv.shape, F32), V((1, 1), F32), dma((6,)), dma((2, chunks)), dma((2, steps)),
+        ],
+        compiler_params=pltpu.CompilerParams(vmem_limit_bytes=GRANT),
+        name="finish",
+    )(views, tapsb, gp.reshape(2, chunks, 4 * depth, piece, wide), conv, total)
     return (
         gfeat.reshape(feats.shape), gproj.reshape(width, deep), gconv.transpose(0, 2, 1),
         loss.reshape(()),

time: 92.4 us -> 68.6 us (0.74)
  Pallas kernels: 80.5 us -> 64.8 us
  local copies, waits for them, and re-layouts: 7.29 us -> 1.37 us
  between operations: 3.1 us -> 1.45 us
    pallas_call x1, Pallas kernels: 80.5 us -> 60.9 us  [local(): pl.pallas_call(functools.partial(step_kernel, slabs, images), out_shape=[...]
    unnamed x5 -> x0, local copies, waits for them, and re-layouts: 6.69 us -> none
    pallas_call x0 -> x1, Pallas kernels: none -> 3.96 us  [local(): pl.pallas_call(finish_kernel, in_specs=[hbm] * 5, out_specs=[hbm] * 4, ou...]
    dynamic_slice x0 -> x1, local copies, waits for them, and re-layouts: none -> 1.37 us  [local(): row = lax.dynamic_slice_in_dim(mod_table, labels[0], 1, 0)]
where the time goes in v2:
time: 68.6 us; the launch traced here: 67.6 us
  Pallas kernels  64.8 us (94%)
  between operations  1.45 us (2%)
  local copies, waits for them, and re-layouts  1.37 us (2%)
    pallas_call x1, Pallas kernels, local(): pl.pallas_call(functools.partial(step_kernel, slabs, images), out_shape=[...  60.9 us
    pallas_call x1, Pallas kernels, local(): pl.pallas_call(finish_kernel, in_specs=[hbm] * 5, out_specs=[hbm] * 4, ou...  3.96 us

profile of v2, /device:TPU:0, one launch (start us, length us, event | category | flops | bytes accessed | tf_op | source)
XLA Modules:
  0.0 67.6 jit_solution(17426219509513629763)
XLA Ops:
  1.3 1.4 %constant_dynamic-slice_fusion.row_hbm = bf16[1,2048]{1,0:T(2,128)(2,1)} fusion(bf16[1000,2048]{1,0:T(8,128)(2,1)} %param.13, s32[]{:T(128)S(6)} %select_n.3), kind=kLoop, calls=%fused_computation | loop fusion | bytes 8196 | tf_op jit(solution)/shard_map/dynamic_slice | solution.py:656
  2.7 60.9 %step.1 = (bf16[48,1024]{1,0:T(8,128)(2,1)}, bf16[48,512]{1,0:T(8,128)(2,1)}, bf16[2,3,2,2,4,32,256]{6,5,4,3,2,1,0:T(8,128)(2,1)}, f32[9,4,512]{2,1,0:T(4,128)}, f32[1,1]{1,0:T(1,128)}) custom-call(bf16[1024,512]{1,0:T(8,128)(2,1)} %bitcast.12, bf16[9,4,512]{2,1,0:T(4,128)(2,1)} %bitcast.14, bf16[16,1024]{1,0:T(8,128)(2,1)} %embed_hbm.1, ...), custom_call_target="tpu_custom_call" | custom-call | tf_op jit(solution)/shard_map/step/pallas_call | solution.py:694
  63.5 4.0 %finish.1 = (bf16[1024,512]{1,0:T(8,128)(2,1)}, f32[1024,768]{1,0:T(8,128)}, f32[9,4,512]{2,1,0:T(4,128)}, f32[1,1]{1,0:T(1,128)}) custom-call(bf16[48,1024]{1,0:T(8,128)(2,1)} %get-tuple-element.13.views_hbm, bf16[48,512]{1,0:T(8,128)(2,1)} %get-tuple-element.14.taps_hbm, bf16[2,3,16,32,256]{4,3,2,1,0:T(8,128)(2,1)} %bitcast.11, ...), custom_call_target="tpu_custom_call" | custom-call | tf_op jit(solution)/shard_map/finish/pallas_call | solution.py:712

commit v3 on v2

--- a/solution.py
+++ b/solution.py
@@ -11,7 +11,7 @@
 PAIR = 2 * HEAD_DIM
 LANES = 128
 TAPS = 48
-GRANT = 60 * 1024 * 1024
+GRANT = 44 * 1024 * 1024
 
 latent_scale = 0.18215
 norm_eps = 1e-06
@@ -64,12 +64,12 @@
 def step_kernel(
     slabs, images,
     feats_hbm, taps_hbm, embed_hbm, row_hbm, qkv_hbm, out_hbm, proj_hbm, dino_hbm,
-    views_hbm, tapsb_hbm, gp_hbm, gconv_hbm, loss_hbm,
+    gfeat_ref, gproj_ref, gconv_ref, loss_ref,
     feats, taps_s, embed_s, row_s, w_own, out_w, proj_w, dino, load_sems,
     taps48, resp_g, terms, terms_all, stack, tokens, emb, xw, tstack, mt, ep,
     inv_s, gct, k_s, v_s, qt, s_s, e_s, r_s, attt, att, residb, gzp, gt_aug, gt, ds_s,
     gk_s, gv_s, gqt, yr, spread, spread_all, vs,
-    cbuf, crecv, cfull, gp, r1, h1, r2, h2, r3, gpo, views_s, gconv_s, loss_s, save_sems, gp_sems,
+    cbuf, crecv, cfull, gp, r1, h1, r2, h2, r3, gpo, loss_s,
     dino_sems, t_send, t_recv, a_send, a_recv, s_send, s_recv,
     c_send, c_recv, d_send, d_recv, p1_sems, p2_sems, p3_send, p3_recv, a3_send, a3_recv,
     a2_sems, a1_sems, a0_sems,
@@ -144,8 +144,6 @@
             vs[kx * 16 + ky * 4 : kx * 16 + ky * 4 + 4, : feats.shape[1]] = (
                 taps_s[ky * 3 + kx].astype(F32))
     taps48[...] = vs[:, : feats.shape[1]].astype(BF16)
-    saves = [pltpu.make_async_copy(taps48, tapsb_hbm, save_sems.at[0])]
-    saves[0].start()
     for dy in range(2):
         for dx in range(2):
             emb[dx * 8 + dy * 4 : dx * 8 + dy * 4 + 4, :] = (
@@ -195,7 +193,7 @@
         ecent, ecent, (((1,), (1,)), ((), ())), precision=lax.Precision.HIGHEST,
         preferred_element_type=F32)
     loads[9].wait()
-    row = row_s[...].astype(F32)
+    row = row_s[...]
     gain = 1.0 + row[:, width:]
     stack_l = jnp.concatenate(
         [emb[...] * gain, gain, row[:, :width], jnp.zeros((6, width), F32)], 0)
@@ -456,12 +454,13 @@
             outs.append(o[h * HEAD_DIM : (h + 1) * HEAD_DIM] * HEAD_DIM ** -0.5)
         gqt[pl.ds(pl.multiple_of(p * PAIR, PAIR), PAIR), :] = jnp.concatenate(outs, 0).astype(BF16)
         for k in ranks:
-            pl.when(p == min(k + 1, npairs - 1))(functools.partial(add1, k))
+            pl.when(p == k)(functools.partial(add1, k))
+        for k in ranks[:2]:
+            pl.when(p == k + 2)(functools.partial(add2, k))
         return 0
 
     lax.fori_loop(0, npairs, backward, 0)
 
-    add2(0)
     def weights(j):
         return jnp.concatenate(split2(xw[j]), 0)
 
@@ -493,11 +492,13 @@
     for c in s_copies:
         c.start()
     spread_all[slab] = spread[pl.ds(slab * strip, strip + 2)]
-    for k in ranks[1:]:
+    for k in ranks[2:]:
         add2(k)
+    add3(0)
     for c in s_copies:
         c.wait_recv()
 
+    add3(1)
     cells = []
     for t in range(strip + 2):
         g = spread_all[0, t]
@@ -518,66 +519,90 @@
         vs[0:16, cut] = shifted(mid_view, -1)
         vs[32:48, cut] = shifted(mid_view, 1)
     views = vs[...].astype(BF16)
-    views_s[...] = views
-    saves.append(pltpu.make_async_copy(views_s, views_hbm, save_sems.at[1]))
-    saves[-1].start()
     conv_part = plain(views, feats[...])
     cbuf[...] = jnp.zeros_like(cbuf)
     for i in range(TAPS // 8):
         for j in range(4):
-            cbuf[i * 4 + j] = conv_part[i * 8 : i * 8 + 8, j * LANES : (j + 1) * LANES]
-    cbuf[TAPS // 2] = jnp.broadcast_to(loss_s[...], (8, LANES))
-    others(devices, me, lambda j: remote(
-        cbuf.at[j], crecv.at[me], c_send.at[j], c_recv.at[me], anyone(j)).start())
-    for k in ranks:
+            cbuf[i * 4 + j] = conv_part[
+                i * 8 : i * 8 + 8, j * LANES : (j + 1) * LANES].astype(BF16)
+    loss_hi, loss_lo = split2(loss_s[...])
+    cbuf[TAPS // 2] = jnp.where(
+        iota((8, LANES), 0) == 0, loss_hi.astype(F32), loss_lo.astype(F32)).astype(BF16)
+    used = TAPS // 2 + 1
+
+    def owners(body):
+        def run(j, _):
+            pl.when(j != me)(lambda: body(j))
+            return 0
+
+        lax.fori_loop(0, used, run, 0)
+
+    def scatter(j):
+        return remote(cbuf.at[j], crecv.at[me], c_send.at[j], c_recv.at[me], anyone(j))
+
+    def share(j):
+        return remote(cfull.at[me], cfull.at[me], d_send.at[j], d_recv.at[me], anyone(j))
+
+    owners(lambda j: scatter(j).start())
+    for k in ranks[2:]:
         add3(k)
-    give3(0)
-    others(devices, me, lambda j: remote(
-        cbuf.at[me], crecv.at[j], c_send.at[j], c_recv.at[j], anyone(j)).wait_recv())
-    total = lax.fori_loop(
-        1, devices, lambda i, acc: acc + crecv[lax.rem(me + i, devices)], cbuf[me])
-    cfull[me] = total
-    others(devices, me, lambda j: remote(
-        cfull.at[me], cfull.at[me], d_send.at[j], d_recv.at[me], anyone(j)).start())
-
+    for i in range(rows * LANES // 256):
+        cut = slice(i * 256, (i + 1) * 256)
+        gfeat_ref[cut, :] = contract_first(views[:, cut], taps48[...]).astype(BF16)
+    for k in ranks[:2]:
+        give3(k)
+
+    @pl.when(me < used)
+    def _():
+        crecv[me] = cbuf[me]
+        others(devices, me, lambda j: remote(
+            cbuf.at[me], crecv.at[j], c_send.at[me], c_recv.at[j], anyone(j)).wait_recv())
+        total = jnp.sum(crecv[...].astype(F32), 0)
+        high = total.astype(BF16)
+        cfull[me, 0] = high
+        cfull[me, 1] = (total - high.astype(F32)).astype(BF16)
+        others(devices, me, lambda j: share(j).start())
+
+    give2(0)
+    for k in ranks[2:]:
+        give3(k)
     for k in ranks[1:]:
-        give3(k)
-    for k in ranks:
         give2(k)
-    others(devices, me, lambda j: remote(
-        cfull.at[me], cfull.at[j], d_send.at[j], d_recv.at[j], anyone(j)).wait_recv())
+    owners(lambda j: remote(
+        cfull.at[j], cfull.at[j], d_send.at[j], d_recv.at[j], anyone(j)).wait_recv())
     for i in range(TAPS // 8):
         for j in range(4):
-            vs[i * 8 : i * 8 + 8, j * LANES : (j + 1) * LANES] = cfull[i * 4 + j]
+            tile = cfull[i * 4 + j].astype(F32)
+            vs[i * 8 : i * 8 + 8, j * LANES : (j + 1) * LANES] = tile[0] + tile[1]
     for kx in range(3):
         for ky in range(3):
-            gconv_s[ky * 3 + kx] = vs[kx * 16 + ky * 4 : kx * 16 + ky * 4 + 4, : 4 * LANES]
-    loss_s[...] = cfull[TAPS // 2, 0:1, 0:1] * (1.0 / (devices * block))
-    saves.append(pltpu.make_async_copy(gconv_s, gconv_hbm, save_sems.at[2]))
-    saves.append(pltpu.make_async_copy(loss_s, loss_hbm, save_sems.at[3]))
-    for c in saves[-2:]:
-        c.start()
+            gconv_ref[ky * 3 + kx] = vs[kx * 16 + ky * 4 : kx * 16 + ky * 4 + 4, : 4 * LANES]
+    tile = cfull[TAPS // 2].astype(F32)
+    tile = tile[0] + tile[1]
+    loss_ref[...] = (tile[0:1, 0:1] + tile[1:2, 0:1]) * (1.0 / (devices * block))
+
+    def store(side, k):
+        gproj_ref[side, :, k * wide : (k + 1) * wide] = (
+            gpo[side, k].astype(F32).reshape(half, wide))
+
     for k in ranks:
         give1(k)
-        saves.append(pltpu.make_async_copy(
-            gpo.at[core, k], gp_hbm.at[core, k], gp_sems.at[0, k]))
-        saves[-1].start()
-    for k in ranks:
-        a0(k, 1 - core).wait_recv()
-        saves.append(pltpu.make_async_copy(
-            gpo.at[1 - core, k], gp_hbm.at[1 - core, k], gp_sems.at[1, k]))
-        saves[-1].start()
-    for c in saves:
-        c.wait()
-
+        store(core, k)
+        if k > 0:
+            a0(k - 1, 1 - core).wait_recv()
+            store(1 - core, k - 1)
+    a0(chunks - 1, 1 - core).wait_recv()
+    store(1 - core, chunks - 1)
     for c in t_copies + s_copies:
         c.wait_send()
     for p in range(npairs):
         att_copy(p).wait_send()
-    others(devices, me, lambda j: remote(
-        cbuf.at[j], crecv.at[me], c_send.at[j], c_recv.at[me], anyone(j)).wait_send())
-    others(devices, me, lambda j: remote(
-        cfull.at[me], cfull.at[me], d_send.at[j], d_recv.at[me], anyone(j)).wait_send())
+    owners(lambda j: scatter(j).wait_send())
+
+    @pl.when(me < used)
+    def _():
+        others(devices, me, lambda j: share(j).wait_send())
+
     for k in ranks:
         p1(k).wait_send()
         p2(k).wait_send()
@@ -588,52 +613,21 @@
         a0(k, core).wait_send()
 
 
-def finish_kernel(
-    views_hbm, taps_hbm, gp_hbm, conv_hbm, sum_hbm, gfeat_hbm, gproj_hbm, gconv_hbm, loss_hbm,
-    views, taps, gp, gfeat, gproj, gconv, loss,
-    load_sems, gp_sems, sems,
-):
-    cores, chunks, many, deep, wide = gp.shape
-    loads = [
-        pltpu.make_async_copy(views_hbm, views, load_sems.at[0]),
-        pltpu.make_async_copy(taps_hbm, taps, load_sems.at[1]),
-    ]
-    parts = [
-        pltpu.make_async_copy(gp_hbm.at[i, k], gp.at[i, k], gp_sems.at[i, k])
-        for i in range(cores) for k in range(chunks)]
-    small = [
-        pltpu.make_async_copy(conv_hbm, gconv, load_sems.at[2]),
-        pltpu.make_async_copy(sum_hbm, loss, load_sems.at[3]),
-    ]
-    for c in loads + small + parts:
-        c.start()
-    for c in loads + small:
-        c.wait()
-    copies = [
-        pltpu.make_async_copy(gconv, gconv_hbm, load_sems.at[4]),
-        pltpu.make_async_copy(loss, loss_hbm, load_sems.at[5]),
-    ]
+def finish_kernel(*refs):
+    count = (len(refs) - 1) // 2
+    sems = refs[-1]
+    pieces = 4
+    copies = []
+    for i in range(count):
+        left, right = refs[i], refs[count + i]
+        cuts = pieces if len(left.shape) == 2 and left.shape[0] > 8 else 1
+        lines = left.shape[0] // cuts
+        for j in range(cuts):
+            copies.append(pltpu.make_async_copy(
+                left.at[j * lines : (j + 1) * lines], right.at[j * lines : (j + 1) * lines],
+                sems.at[i, j]))
     for c in copies:
         c.start()
-    lines = gfeat.shape[1]
-    for i in range(gfeat.shape[0]):
-        gfeat[i] = contract_first(
-            views[:, i * lines : (i + 1) * lines], taps[...]).astype(BF16)
-        copies.append(pltpu.make_async_copy(
-            gfeat.at[i], gfeat_hbm.at[pl.ds(i * lines, lines)], sems.at[0, i]))
-        copies[-1].start()
-    blocks = gproj.shape[0] // cores
-    each = many // blocks
-    lines = each * deep
-    for i in range(cores * blocks):
-        for k in range(chunks):
-            if i % blocks == 0:
-                parts[i // blocks * chunks + k].wait()
-            cut = gp[i // blocks, k, i % blocks * each : (i % blocks + 1) * each]
-            gproj[i, :, k * wide : (k + 1) * wide] = cut.astype(F32).reshape(lines, wide)
-        copies.append(pltpu.make_async_copy(
-            gproj.at[i], gproj_hbm.at[pl.ds(i * lines, lines)], sems.at[1, i]))
-        copies[-1].start()
     for c in copies:
         c.wait()
 
@@ -653,18 +647,19 @@
     pairs = half // PAIR
     features = embed_w.shape[0]
     taps = conv_w.transpose(0, 2, 1)
-    row = lax.dynamic_slice_in_dim(mod_table, labels[0], 1, 0)
+    row = lax.dynamic_slice_in_dim(mod_table, labels[0], 1, 0).astype(F32)
     depth = images // 2
     wide = 2 * LANES
     piece = half // (4 * depth)
     chunks = deep // wide
     hbm = pl.BlockSpec(memory_space=pltpu.HBM)
+    vmem = pl.BlockSpec(memory_space=pltpu.VMEM)
     dma = pltpu.SemaphoreType.DMA
     strip = block // LANES
     V = pltpu.VMEM
     scratch = [
         V((rows * cols, chans), BF16), V(taps.shape, BF16), V(embed_w.shape, BF16),
-        V((1, 2 * width), BF16), V((3, width, half), BF16), V((width, width), BF16),
+        V((1, 2 * width), F32), V((3, width, half), BF16), V((width, width), BF16),
         V((width, deep), BF16), V((2, block, deep), BF16), dma((11,)),
         V((TAPS, chans), BF16), V((rows, 16, LANES), F32), V((rows // 2 + 2, 8, LANES), F32),
         V((slabs, rows // 2 + 2, 8, LANES), F32), V((rows * slabs // 4 * 8, 2 * LANES), F32),
@@ -679,55 +674,44 @@
         V((pairs, full, PAIR), BF16), V((pairs, full, PAIR), BF16), V((half, own), BF16),
         V((features, own), F32), V((full // LANES + 2, features, LANES), F32),
         V((slabs, strip + 2, features, LANES), F32), V((TAPS, rows * cols), F32),
-        V((devices, 8, LANES), F32), V((devices, 8, LANES), F32), V((devices, 8, LANES), F32),
+        V((devices, 8, LANES), BF16), V((devices, 8, LANES), BF16), V((devices, 2, 8, LANES), BF16),
         V((chunks, 2, 2, depth, piece, wide), BF16), V((chunks, 2, depth, piece, wide), BF16),
         V((chunks, 2, depth, piece, wide), BF16), V((chunks, depth, piece, wide), BF16),
         V((chunks, depth, piece, wide), BF16), V((chunks, depth, piece, wide), BF16),
-        V((2, chunks, 2, 2, depth, piece, wide), BF16), V((TAPS, rows * cols), BF16),
-        V((9, conv_w.shape[2], chans), F32), V((1, 1), F32), dma((4,)), dma((2, chunks)),
+        V((2, chunks, 2, 2, depth, piece, wide), BF16), V((1, 1), F32),
         dma((2,)), dma((slabs,)), dma((slabs,)), dma((pairs,)), dma((pairs,)),
         dma((slabs,)), dma((slabs,)), dma((devices,)), dma((devices,)), dma((devices,)),
         dma((devices,)), dma((2, chunks)), dma((2, chunks)), dma((chunks, depth)),
         dma((chunks, depth)), dma((chunks, depth)), dma((chunks, depth)), dma((2, chunks)),
         dma((2, chunks)), dma((2, chunks)),
     ]
-    views, tapsb, gp, conv, total = pl.pallas_call(
+    shapes = [
+        jax.ShapeDtypeStruct((rows * cols, chans), BF16),
+        jax.ShapeDtypeStruct((2, half, deep), F32),
+        jax.ShapeDtypeStruct((9, conv_w.shape[2], chans), F32),
+        jax.ShapeDtypeStruct((1, 1), F32),
+    ]
+    given = (feats.reshape(rows * cols, chans), taps, embed_w, row, qkv_w, out_w, proj_w, dino[0])
+    made = pl.pallas_call(
         functools.partial(step_kernel, slabs, images),
-        out_shape=[
-            jax.ShapeDtypeStruct((TAPS, rows * cols), BF16),
-            jax.ShapeDtypeStruct((TAPS, chans), BF16),
-            jax.ShapeDtypeStruct((2, chunks, 2, 2, depth, piece, wide), BF16),
-            jax.ShapeDtypeStruct((9, conv_w.shape[2], chans), F32),
-            jax.ShapeDtypeStruct((1, 1), F32),
-        ],
+        out_shape=shapes,
         in_specs=[hbm] * 8,
-        out_specs=[hbm] * 5,
+        out_specs=[vmem] * 4,
         scratch_shapes=scratch,
         compiler_params=pltpu.CompilerParams(
             collective_id=0, has_side_effects=True, vmem_limit_bytes=GRANT),
         name="step",
-    )(feats.reshape(rows * cols, chans), taps, embed_w, row, qkv_w, out_w, proj_w,
-      dino[0])
-    steps = 4
+    )(*[pltpu.with_memory_space_constraint(x, pltpu.HBM) for x in given])
+    made = [made[0], made[1].reshape(width, deep), made[2], made[3]]
     gfeat, gproj, gconv, loss = pl.pallas_call(
         finish_kernel,
-        in_specs=[hbm] * 5,
+        in_specs=[vmem] * 4,
         out_specs=[hbm] * 4,
-        out_shape=[
-            jax.ShapeDtypeStruct((rows * cols, chans), BF16),
-            jax.ShapeDtypeStruct((width, deep), F32),
-            jax.ShapeDtypeStruct(conv.shape, F32),
-            jax.ShapeDtypeStruct((1, 1), F32),
-        ],
-        scratch_shapes=[
-            V((TAPS, rows * cols), BF16), V((TAPS, chans), BF16),
-            V((2, chunks, 4 * depth, piece, wide), BF16),
-            V((steps, rows * cols // steps, chans), BF16), V((steps, width // steps, deep), F32),
-            V(conv.shape, F32), V((1, 1), F32), dma((6,)), dma((2, chunks)), dma((2, steps)),
-        ],
-        compiler_params=pltpu.CompilerParams(vmem_limit_bytes=GRANT),
+        out_shape=[jax.ShapeDtypeStruct(m.shape, m.dtype) for m in made],
+        scratch_shapes=[dma((4, 4))],
+        compiler_params=pltpu.CompilerParams(vmem_limit_bytes=8 * 1024 * 1024),
         name="finish",
-    )(views, tapsb, gp.reshape(2, chunks, 4 * depth, piece, wide), conv, total)
+    )(*made)
     return (
         gfeat.reshape(feats.shape), gproj.reshape(width, deep), gconv.transpose(0, 2, 1),
         loss.reshape(()),

time: 68.6 us -> 64 us (0.933)
  Pallas kernels: 64.8 us -> 60.2 us
  other arithmetic: 0 us -> 1.37 us
  local copies, waits for them, and re-layouts: 1.37 us -> 0 us
    pallas_call x2, Pallas kernels: 64.8 us -> 60.2 us  [the longest x1 57.4 us: local(): pl.pallas_call(functools.partial(step_kernel, slabs, images), out_shape=s...]
    dynamic_slice x1 -> x0, local copies, waits for them, and re-layouts: 1.37 us -> none  [local(): row = lax.dynamic_slice_in_dim(mod_table, labels[0], 1, 0)]
    convert_element_type x0 -> x1, other arithmetic: none -> 1.37 us  [local(): row = lax.dynamic_slice_in_dim(mod_table, labels[0], 1, 0).astype(F32)]
where the time goes in v3:
time: 64 us; the launch traced here: 63 us
  Pallas kernels  60.2 us (94%)
  between operations  1.45 us (2%)
  other arithmetic  1.37 us (2%)
    pallas_call x1, Pallas kernels, local(): pl.pallas_call(functools.partial(step_kernel, slabs, images), out_shape=s...  57.4 us
    pallas_call x1, Pallas kernels, local(): pl.pallas_call(finish_kernel, in_specs=[vmem] * 4, out_specs=[hbm] * 4, o...  2.79 us
    convert_element_type x1, other arithmetic, local(): row = lax.dynamic_slice_in_dim(mod_table, labels[0], 1, 0).astype(F32)  1.37 us

profile of v3, /device:TPU:0, one launch (start us, length us, event | category | flops | bytes accessed | tf_op | source)
XLA Modules:
  0.0 63.0 jit_solution(13580058476234534390)
XLA Ops:
  1.3 1.4 %dynamic-slice_convert_fusion.row_hbm = f32[1,2048]{1,0:T(1,128)} fusion(bf16[1000,2048]{1,0:T(8,128)(2,1)} %param.13, s32[]{:T(128)S(6)} %select_n.3), kind=kLoop, calls=%fused_computation | loop fusion | flops 2048 | bytes 12292 | tf_op jit(solution)/shard_map/convert_element_type | solution.py:650
  2.6 57.4 %step.1 = (bf16[1024,512]{1,0:T(8,128)(2,1)S(1)}, f32[2,512,768]{2,1,0:T(8,128)S(1)}, f32[9,4,512]{2,1,0:T(4,128)S(1)}, f32[1,1]{1,0:T(1,128)}) custom-call(bf16[1024,512]{1,0:T(8,128)(2,1)} %bitcast.12, bf16[9,4,512]{2,1,0:T(4,128)(2,1)} %bitcast.14, bf16[16,1024]{1,0:T(8,128)(2,1)} %embed_hbm.1, f32[1,2048]{1,0:T(1,128)} %dynamic-slice_convert_fusion.row_hbm, ...), custom_call_target="tpu_custom_call" | custom-call | tf_op jit(solution)/shard_map/step/pallas_call | solution.py:695
  60.1 2.8 %finish.1 = (bf16[1024,512]{1,0:T(8,128)(2,1)}, f32[1024,768]{1,0:T(8,128)}, f32[9,4,512]{2,1,0:T(4,128)}, f32[1,1]{1,0:T(1,128)}) custom-call(bf16[1024,512]{1,0:T(8,128)(2,1)S(1)} %get-tuple-element.12.refs_0_, f32[1024,768]{1,0:T(8,128)S(1)} %bitcast.11, f32[9,4,512]{2,1,0:T(4,128)S(1)} %get-tuple-element.14.refs_2_, f32[1,1]{1,0:T(1,128)} %get-tuple-element.15.refs_3_), custom_call_target="tpu_custom_call" | custom-call | tf_op jit(solution)/shard_map/finish/pallas_call | solution.py:706

commit v4 on v3

--- a/solution.py
+++ b/solution.py
@@ -174,7 +174,7 @@
     for d in range(1, slabs):
         peer = lax.rem(slab + d, slabs)
         t_copies.append(remote(
-            terms, terms_all.at[slab], t_send.at[d], t_recv.at[d], {"slab": peer, "img": image}))
+            terms, terms_all.at[slab], t_send, t_recv, {"slab": peer, "img": image}))
     for c in t_copies:
         c.start()
     loads[6].wait()
@@ -203,8 +203,10 @@
         prod = plain(parts, w_own[j])
         xw[j] = prod[0:24] + prod[24:48] + prod[48:72]
 
-    for c in t_copies:
-        c.wait_recv()
+    few = slabs - 1
+    halo_wait = remote(
+        terms_all.at[pl.ds(0, few)], terms_all.at[pl.ds(0, few)], t_send, t_recv, partner)
+    halo_wait.wait_recv()
 
     per = rows // 2
     for i in range(per * slabs):
@@ -279,7 +281,7 @@
         qt[2 * p + 1] = jnp.concatenate([blank, qq[p * PAIR + HEAD_DIM : (p + 1) * PAIR]], 0)
 
     def att_copy(p):
-        return remote(att.at[core, p], att.at[core, p], a_send.at[p], a_recv.at[p], partner)
+        return remote(att.at[core, p], att.at[core, p], a_send, a_recv, partner)
 
     units = [(p, b, h) for p in range(npairs) for b in range(own // 256) for h in range(2)]
 
@@ -317,9 +319,9 @@
             gather(i - 1, kept)
         top = later
     loads[10].wait()
-    dino_copy.wait()
-    for p in range(npairs):
-        att_copy(p).wait_recv()
+    dino_copy.wait_recv()
+    att_wait = remote(att.at[core], att.at[core], a_send, a_recv, partner)
+    att_wait.wait_recv()
 
     spread[...] = jnp.zeros_like(spread)
     loss_s[...] = jnp.zeros_like(loss_s)
@@ -351,32 +353,39 @@
     ranks = range(chunks)
 
     def p1(k):
-        return remote(gp.at[k, 1 - first], r1.at[k], p1_sems.at[0, k], p1_sems.at[1, k], hop1)
+        return remote(gp.at[k, 1 - first], r1.at[k], p1_sems.at[chunks], p1_sems.at[k], hop1)
 
     def p2(k):
-        return remote(h1.at[k, 1 - second], r2.at[k], p2_sems.at[0, k], p2_sems.at[1, k], hop2)
-
-    def p3(k, j, slot, sem):
-        return remote(h2.at[k, j], r3.at[k, slot], p3_send.at[k, j], p3_recv.at[k, sem], level(j))
-
-    def a3(k, j, slot):
-        return remote(
-            gpo.at[core, k, first, second, north], gpo.at[core, k, first, second, slot],
-            a3_send.at[k, j], a3_recv.at[k, slot], level(j))
+        return remote(h1.at[k, 1 - second], r2.at[k], p2_sems.at[chunks], p2_sems.at[k], hop2)
+
+    def p3(k, j):
+        return remote(h2.at[k, j], r3.at[k, north], p3_send, p3_recv.at[k], level(j))
+
+    def p3_wait(k):
+        some = r3.at[k, pl.ds(0, depth - 1)]
+        return remote(some, some, p3_send, p3_recv.at[k], partner)
+
+    def a3(k, j):
+        mine = gpo.at[core, k, first, second, north]
+        return remote(mine, mine, a3_send, a3_recv.at[k], level(j))
+
+    def a3_wait(k):
+        some = gpo.at[core, k, first, second, pl.ds(0, depth - 1)]
+        return remote(some, some, a3_send, a3_recv.at[k], partner)
 
     def a2(k, there):
         return remote(
             gpo.at[core, k, first, second], gpo.at[core, k, first, there],
-            a2_sems.at[0, k], a2_sems.at[1, k], hop2)
+            a2_sems.at[chunks], a2_sems.at[k], hop2)
 
     def a1(k, there):
         return remote(
             gpo.at[core, k, first], gpo.at[core, k, there],
-            a1_sems.at[0, k], a1_sems.at[1, k], hop1)
+            a1_sems.at[chunks], a1_sems.at[k], hop1)
 
     def a0(k, there):
         return remote(
-            gpo.at[core, k], gpo.at[there, k], a0_sems.at[0, k], a0_sems.at[1, k], partner)
+            gpo.at[core, k], gpo.at[there, k], a0_sems.at[chunks], a0_sems.at[k], partner)
 
     def add1(k):
         p1(k).wait_recv()
@@ -386,18 +395,18 @@
     def add2(k):
         p2(k).wait_recv()
         h2[k] = (h1[k, second].astype(F32) + r2[k].astype(F32)).astype(BF16)
-        others(depth, north, lambda j: p3(k, j, north, north).start())
+        others(depth, north, lambda j: p3(k, j).start())
 
     def add3(k):
-        others(depth, north, lambda j: p3(k, j, j, j).wait_recv())
+        p3_wait(k).wait_recv()
         total = lax.fori_loop(
             1, depth, lambda i, acc: acc + r3[k, lax.rem(north + i, depth)].astype(F32),
             h2[k, north].astype(F32))
         gpo[core, k, first, second, north] = total.astype(BF16)
-        others(depth, north, lambda j: a3(k, j, north).start())
+        others(depth, north, lambda j: a3(k, j).start())
 
     def give3(k):
-        others(depth, north, lambda j: a3(k, j, j).wait_recv())
+        a3_wait(k).wait_recv()
         a2(k, second).start()
 
     def give2(k):
@@ -488,15 +497,16 @@
         peer = lax.rem(slab + d, slabs)
         s_copies.append(remote(
             spread.at[pl.ds(peer * strip, strip + 2)], spread_all.at[slab],
-            s_send.at[d], s_recv.at[d], {"slab": peer, "img": image}))
+            s_send, s_recv, {"slab": peer, "img": image}))
     for c in s_copies:
         c.start()
     spread_all[slab] = spread[pl.ds(slab * strip, strip + 2)]
     for k in ranks[2:]:
         add2(k)
     add3(0)
-    for c in s_copies:
-        c.wait_recv()
+    back_wait = remote(
+        spread_all.at[pl.ds(0, few)], spread_all.at[pl.ds(0, few)], s_send, s_recv, partner)
+    back_wait.wait_recv()
 
     add3(1)
     cells = []
@@ -538,10 +548,17 @@
         lax.fori_loop(0, used, run, 0)
 
     def scatter(j):
-        return remote(cbuf.at[j], crecv.at[me], c_send.at[j], c_recv.at[me], anyone(j))
+        return remote(cbuf.at[j], crecv.at[me], c_send, c_recv, anyone(j))
+
+    def tiles_of(ref, count, send, recv):
+        return remote(ref.at[pl.ds(0, count)], ref.at[pl.ds(0, count)], send, recv, partner)
+
+    def by_role(body):
+        pl.when(me < used)(lambda: body(used - 1))
+        pl.when(me >= used)(lambda: body(used))
 
     def share(j):
-        return remote(cfull.at[me], cfull.at[me], d_send.at[j], d_recv.at[me], anyone(j))
+        return remote(cfull.at[me], cfull.at[me], d_send, d_recv, anyone(j))
 
     owners(lambda j: scatter(j).start())
     for k in ranks[2:]:
@@ -555,8 +572,7 @@
     @pl.when(me < used)
     def _():
         crecv[me] = cbuf[me]
-        others(devices, me, lambda j: remote(
-            cbuf.at[me], crecv.at[j], c_send.at[me], c_recv.at[j], anyone(j)).wait_recv())
+        tiles_of(crecv, devices - 1, c_send, c_recv).wait_recv()
         total = jnp.sum(crecv[...].astype(F32), 0)
         high = total.astype(BF16)
         cfull[me, 0] = high
@@ -568,8 +584,16 @@
         give3(k)
     for k in ranks[1:]:
         give2(k)
-    owners(lambda j: remote(
-        cfull.at[j], cfull.at[j], d_send.at[j], d_recv.at[j], anyone(j)).wait_recv())
+    halo_wait.wait_send()
+    dino_copy.wait_send()
+    att_wait.wait_send()
+    back_wait.wait_send()
+    by_role(lambda count: tiles_of(cbuf, count, c_send, c_recv).wait_send())
+    remote(r1, r1, p1_sems.at[chunks], p1_sems.at[0], partner).wait_send()
+    remote(r2, r2, p2_sems.at[chunks], p2_sems.at[0], partner).wait_send()
+    every = r3.at[:, pl.ds(0, depth - 1)]
+    remote(every, every, p3_send, p3_recv.at[0], partner).wait_send()
+    by_role(lambda count: tiles_of(cfull, count, d_send, d_recv).wait_recv())
     for i in range(TAPS // 8):
         for j in range(4):
             tile = cfull[i * 4 + j].astype(F32)
@@ -593,24 +617,17 @@
             store(1 - core, k - 1)
     a0(chunks - 1, 1 - core).wait_recv()
     store(1 - core, chunks - 1)
-    for c in t_copies + s_copies:
-        c.wait_send()
-    for p in range(npairs):
-        att_copy(p).wait_send()
-    owners(lambda j: scatter(j).wait_send())
-
     @pl.when(me < used)
     def _():
-        others(devices, me, lambda j: share(j).wait_send())
-
-    for k in ranks:
-        p1(k).wait_send()
-        p2(k).wait_send()
-        others(depth, north, lambda j, k=k: p3(k, j, north, north).wait_send())
-        others(depth, north, lambda j, k=k: a3(k, j, north).wait_send())
-        a2(k, second).wait_send()
-        a1(k, first).wait_send()
-        a0(k, core).wait_send()
+        tiles_of(cfull, devices - 1, d_send, d_recv).wait_send()
+
+    for ref, send, recv in (
+        (gpo.at[core, :, first, second, pl.ds(0, depth - 1)], a3_send, a3_recv.at[0]),
+        (gpo.at[core, :, first, second], a2_sems.at[chunks], a2_sems.at[0]),
+        (gpo.at[core, :, first], a1_sems.at[chunks], a1_sems.at[0]),
+        (gpo.at[core], a0_sems.at[chunks], a0_sems.at[0]),
+    ):
+        remote(ref, ref, send, recv, partner).wait_send()
 
 
 def finish_kernel(*refs):
@@ -679,11 +696,9 @@
         V((chunks, 2, depth, piece, wide), BF16), V((chunks, depth, piece, wide), BF16),
         V((chunks, depth, piece, wide), BF16), V((chunks, depth, piece, wide), BF16),
         V((2, chunks, 2, 2, depth, piece, wide), BF16), V((1, 1), F32),
-        dma((2,)), dma((slabs,)), dma((slabs,)), dma((pairs,)), dma((pairs,)),
-        dma((slabs,)), dma((slabs,)), dma((devices,)), dma((devices,)), dma((devices,)),
-        dma((devices,)), dma((2, chunks)), dma((2, chunks)), dma((chunks, depth)),
-        dma((chunks, depth)), dma((chunks, depth)), dma((chunks, depth)), dma((2, chunks)),
-        dma((2, chunks)), dma((2, chunks)),
+        dma((2,)), dma, dma, dma, dma, dma, dma, dma, dma, dma, dma, dma((chunks + 1,)),
+        dma((chunks + 1,)), dma, dma((chunks,)), dma, dma((chunks,)), dma((chunks + 1,)),
+        dma((chunks + 1,)), dma((chunks + 1,)),
     ]
     shapes = [
         jax.ShapeDtypeStruct((rows * cols, chans), BF16),

time: 64 us -> 61.4 us (0.959); the launches traced: 63 us -> 61.2 us
  Pallas kernels: 60.2 us -> 58.4 us
    pallas_call x1, Pallas kernels: 57.4 us -> 55.6 us  [local(): pl.pallas_call(functools.partial(step_kernel, slabs, images), out_shape=s...]
where the time goes in v4:
time: 61.4 us; the launch traced here: 61.2 us
  Pallas kernels  58.4 us (95%)
  between operations  1.45 us (2%)
  other arithmetic  1.37 us (2%)
    pallas_call x1, Pallas kernels, local(): pl.pallas_call(functools.partial(step_kernel, slabs, images), out_shape=s...  55.6 us
    pallas_call x1, Pallas kernels, local(): pl.pallas_call(finish_kernel, in_specs=[vmem] * 4, out_specs=[hbm] * 4, o...  2.79 us
    convert_element_type x1, other arithmetic, local(): row = lax.dynamic_slice_in_dim(mod_table, labels[0], 1, 0).astype(F32)  1.37 us

profile of v4, /device:TPU:0, one launch (start us, length us, event | category | flops | bytes accessed | tf_op | source)
XLA Modules:
  0.0 61.2 jit_solution(3341555926238259687)
XLA Ops:
  1.3 1.4 %dynamic-slice_convert_fusion.row_hbm = f32[1,2048]{1,0:T(1,128)} fusion(bf16[1000,2048]{1,0:T(8,128)(2,1)} %param.13, s32[]{:T(128)S(6)} %select_n.3), kind=kLoop, calls=%fused_computation | loop fusion | flops 2048 | bytes 12292 | tf_op jit(solution)/shard_map/convert_element_type | solution.py:667
  2.6 55.6 %step.1 = (bf16[1024,512]{1,0:T(8,128)(2,1)S(1)}, f32[2,512,768]{2,1,0:T(8,128)S(1)}, f32[9,4,512]{2,1,0:T(4,128)S(1)}, f32[1,1]{1,0:T(1,128)}) custom-call(bf16[1024,512]{1,0:T(8,128)(2,1)} %bitcast.12, bf16[9,4,512]{2,1,0:T(4,128)(2,1)} %bitcast.14, bf16[16,1024]{1,0:T(8,128)(2,1)} %embed_hbm.1, f32[1,2048]{1,0:T(1,128)} %dynamic-slice_convert_fusion.row_hbm, ...), custom_call_target="tpu_custom_call" | custom-call | tf_op jit(solution)/shard_map/step/pallas_call | solution.py:710
  58.3 2.8 %finish.1 = (bf16[1024,512]{1,0:T(8,128)(2,1)}, f32[1024,768]{1,0:T(8,128)}, f32[9,4,512]{2,1,0:T(4,128)}, f32[1,1]{1,0:T(1,128)}) custom-call(bf16[1024,512]{1,0:T(8,128)(2,1)S(1)} %get-tuple-element.12.refs_0_, f32[1024,768]{1,0:T(8,128)S(1)} %bitcast.11, f32[9,4,512]{2,1,0:T(4,128)S(1)} %get-tuple-element.14.refs_2_, f32[1,1]{1,0:T(1,128)} %get-tuple-element.15.refs_3_), custom_call_target="tpu_custom_call" | custom-call | tf_op jit(solution)/shard_map/finish/pallas_call | solution.py:721

commit v5 on v4

--- a/solution.py
+++ b/solution.py
@@ -67,7 +67,7 @@
     gfeat_ref, gproj_ref, gconv_ref, loss_ref,
     feats, taps_s, embed_s, row_s, w_own, out_w, proj_w, dino, load_sems,
     taps48, resp_g, terms, terms_all, stack, tokens, emb, xw, tstack, mt, ep,
-    inv_s, gct, k_s, v_s, qt, s_s, e_s, r_s, attt, att, residb, gzp, gt_aug, gt, ds_s,
+    inv_s, gct, k_s, v_s, qt, s_s, e_s, r_s, attt, att, base, residb, gzp, gt_aug, gt, ds_s,
     gk_s, gv_s, gqt, yr, spread, spread_all, vs,
     cbuf, crecv, cfull, gp, r1, h1, r2, h2, r3, gpo, loss_s,
     dino_sems, t_send, t_recv, a_send, a_recv, s_send, s_recv,
@@ -318,35 +318,35 @@
         if i > 0:
             gather(i - 1, kept)
         top = later
+    tstack[0:48, :] = tok3
+    cuts = [slice(b * 256, (b + 1) * 256) for b in range(own // 256)]
+
+    def outward(side, cut):
+        a = jnp.concatenate([att[side, p, cut, :] for p in range(npairs)], 1)
+        return plain(a, out_w[pl.ds(pl.multiple_of(side * half, 8), half), :])
+
+    for b, cut in enumerate(cuts):
+        piece = pl.ds(pl.multiple_of(chip * own + b * 256, LANES), 256)
+        base[cut, :] = contract_first(tstack[0:48, piece], emb3) + outward(core, cut)
+    spread[...] = jnp.zeros_like(spread)
+    vs[...] = jnp.zeros_like(vs)
+    ep_parts = jnp.concatenate(split2(ep[...]), 0)
     loads[10].wait()
     dino_copy.wait_recv()
     att_wait = remote(att.at[core], att.at[core], a_send, a_recv, partner)
     att_wait.wait_recv()
-
-    spread[...] = jnp.zeros_like(spread)
-    loss_s[...] = jnp.zeros_like(loss_s)
-    vs[...] = jnp.zeros_like(vs)
-    tstack[0:48, :] = tok3
-    ep_parts = jnp.concatenate(split2(ep[...]), 0)
-
-    def middle(b, _):
-        line = pl.ds(pl.multiple_of(b * 256, 256), 256)
-        piece = pl.ds(pl.multiple_of(chip * own + b * 256, LANES), 256)
-        a = jnp.concatenate([att[i, p, line, :] for i in range(2) for p in range(npairs)], 1)
-        resid = contract_first(tstack[0:48, piece], emb3) + plain(a, out_w[...])
-        rb = resid.astype(BF16)
-        residb[line, :] = rb
+    loss = jnp.zeros((1, 1), F32)
+    for b, cut in enumerate(cuts):
+        rb = (base[cut, :] + outward(1 - core, cut)).astype(BF16)
+        residb[cut, :] = rb
         zp = plain(rb, proj_w[...])
         d = dino[b].astype(F32)
         norm_p = jnp.sqrt(jnp.sum(zp * zp, -1, keepdims=True) + cosine_eps)
         norm_t = jnp.sqrt(jnp.sum(d * d, -1, keepdims=True) + cosine_eps)
         cos = jnp.sum(zp * d, -1, keepdims=True) / (norm_p * norm_t)
-        g = (zp * (cos / (norm_p * norm_p)) - d / (norm_p * norm_t)).astype(BF16)
-        gzp[line, :] = g
-        loss_s[...] += jnp.sum(1.0 - cos, 0, keepdims=True) * 0.5
-        return 0
-
-    lax.fori_loop(0, own // 256, middle, 0)
+        gzp[cut, :] = (zp * (cos / (norm_p * norm_p)) - d / (norm_p * norm_t)).astype(BF16)
+        loss = loss + jnp.sum(1.0 - cos, 0, keepdims=True) * 0.5
+    loss_s[...] = loss
 
     rh = residb[:, pl.ds(pl.multiple_of(core * half, LANES), half)]
     chunks, wide = gp.shape[0], gp.shape[-1]
@@ -383,9 +383,13 @@
             gpo.at[core, k, first], gpo.at[core, k, there],
             a1_sems.at[chunks], a1_sems.at[k], hop1)
 
-    def a0(k, there):
-        return remote(
-            gpo.at[core, k], gpo.at[there, k], a0_sems.at[chunks], a0_sems.at[k], partner)
+    def a0(k, part):
+        some = gpo.at[core, k, part]
+        return remote(some, some, a0_sems.at[chunks], a0_sems.at[k], partner)
+
+    def a0_wait(k):
+        some = gpo.at[1 - core, k]
+        return remote(some, some, a0_sems.at[chunks], a0_sems.at[k], partner)
 
     def add1(k):
         p1(k).wait_recv()
@@ -412,10 +416,11 @@
     def give2(k):
         a2(k, 1 - second).wait_recv()
         a1(k, first).start()
+        a0(k, first).start()
 
     def give1(k):
         a1(k, 1 - first).wait_recv()
-        a0(k, core).start()
+        a0(k, 1 - first).start()
 
     for k in ranks:
         part = contract_first(rh, gzp[:, k * wide : (k + 1) * wide]).astype(BF16)
@@ -613,9 +618,9 @@
         give1(k)
         store(core, k)
         if k > 0:
-            a0(k - 1, 1 - core).wait_recv()
+            a0_wait(k - 1).wait_recv()
             store(1 - core, k - 1)
-    a0(chunks - 1, 1 - core).wait_recv()
+    a0_wait(chunks - 1).wait_recv()
     store(1 - core, chunks - 1)
     @pl.when(me < used)
     def _():
@@ -685,7 +690,7 @@
         V((1, full), F32), V((features, full), F32), V((pairs, full, PAIR), BF16),
         V((heads, full, PAIR), BF16), V((heads, PAIR, own), BF16), V((3, full, 256), F32),
         V((heads, full, own), BF16),
-        V((pairs, 2, own), F32), V((pairs, PAIR, own), BF16), V((2, pairs, own, PAIR), BF16),
+        V((pairs, 2, own), F32), V((pairs, PAIR, own), BF16), V((2, pairs, own, PAIR), BF16), V((own, width), F32),
         V((own, width), BF16), V((own, deep), BF16), V((heads, PAIR, own), BF16),
         V((heads, PAIR, own), BF16), V((2, full, own), BF16),
         V((pairs, full, PAIR), BF16), V((pairs, full, PAIR), BF16), V((half, own), BF16),

time: 61.4 us -> 59.8 us (0.974)
  Pallas kernels: 58.4 us -> 56.8 us
    pallas_call x1, Pallas kernels: 55.6 us -> 54 us  [local(): pl.pallas_call(functools.partial(step_kernel, slabs, images), out_shape=s...]
where the time goes in v5:
time: 59.8 us; the launch traced here: 59.6 us
  Pallas kernels  56.8 us (95%)
  between operations  1.45 us (2%)
  other arithmetic  1.37 us (2%)
    pallas_call x1, Pallas kernels, local(): pl.pallas_call(functools.partial(step_kernel, slabs, images), out_shape=s...  54 us
    pallas_call x1, Pallas kernels, local(): pl.pallas_call(finish_kernel, in_specs=[vmem] * 4, out_specs=[hbm] * 4, o...  2.79 us
    convert_element_type x1, other arithmetic, local(): row = lax.dynamic_slice_in_dim(mod_table, labels[0], 1, 0).astype(F32)  1.37 us

profile of v5, /device:TPU:0, one launch (start us, length us, event | category | flops | bytes accessed | tf_op | source)
XLA Modules:
  0.0 59.6 jit_solution(8195875093398043905)
XLA Ops:
  1.3 1.4 %dynamic-slice_convert_fusion.row_hbm = f32[1,2048]{1,0:T(1,128)} fusion(bf16[1000,2048]{1,0:T(8,128)(2,1)} %param.13, s32[]{:T(128)S(6)} %select_n.3), kind=kLoop, calls=%fused_computation | loop fusion | flops 2048 | bytes 12292 | tf_op jit(solution)/shard_map/convert_element_type | solution.py:672
  2.6 54.0 %step.1 = (bf16[1024,512]{1,0:T(8,128)(2,1)S(1)}, f32[2,512,768]{2,1,0:T(8,128)S(1)}, f32[9,4,512]{2,1,0:T(4,128)S(1)}, f32[1,1]{1,0:T(1,128)}) custom-call(bf16[1024,512]{1,0:T(8,128)(2,1)} %bitcast.12, bf16[9,4,512]{2,1,0:T(4,128)(2,1)} %bitcast.14, bf16[16,1024]{1,0:T(8,128)(2,1)} %embed_hbm.1, f32[1,2048]{1,0:T(1,128)} %dynamic-slice_convert_fusion.row_hbm, ...), custom_call_target="tpu_custom_call" | custom-call | tf_op jit(solution)/shard_map/step/pallas_call | solution.py:715
  56.7 2.8 %finish.1 = (bf16[1024,512]{1,0:T(8,128)(2,1)}, f32[1024,768]{1,0:T(8,128)}, f32[9,4,512]{2,1,0:T(4,128)}, f32[1,1]{1,0:T(1,128)}) custom-call(bf16[1024,512]{1,0:T(8,128)(2,1)S(1)} %get-tuple-element.12.refs_0_, f32[1024,768]{1,0:T(8,128)S(1)} %bitcast.11, f32[9,4,512]{2,1,0:T(4,128)S(1)} %get-tuple-element.14.refs_2_, f32[1,1]{1,0:T(1,128)} %get-tuple-element.15.refs_3_), custom_call_target="tpu_custom_call" | custom-call | tf_op jit(solution)/shard_map/finish/pallas_call | solution.py:726
